TPU v7x, 32 devices: a whole 2x2x4 slice. The times are simulated.
32 devices in a mesh: row: 2 (over core), sector: 4 (over z), slab: 4 (over y, x).
Axes of the slice: x: 2, y: 2, z: 4, core: 2. Of those that a mesh axis runs over, the one named last changes fastest.
Arguments:
- state: float32 [2, 5, 32, 128, 128], P('row', None, 'slab', 'sector'), may hold values from -6 to 6
- source: float32 [2, 5, 32, 128, 128], P('row', None, 'slab', 'sector'), may hold values from -6 to 6
- diag_inverse: float32 [2, 5, 5, 32, 128, 128], P('row', None, None, 'slab', 'sector'), may hold values from -1 to 1
- jac_axial: float32 [2, 5, 5], P('row'), may hold values from -1 to 2
- jac_cross: float32 [2, 2, 5, 5], P('row'), may hold values from -2.5 to 2.5
- owner: int32 [128], replicated, may hold values from 0 to 127, as said below
Outputs:
- residual: float32 [2, 5, 32, 128, 128], P('row', None, 'slab', 'sector')
- new_state: float32 [2, 5, 32, 128, 128], P('row', None, 'slab', 'sector')
Inputs may be any that keep to these rules, and one draw needn't show every extreme that they name: owner is a permutation; for some whole s, the columns b * 32 to b * 32 + 31 of the rotor face exactly the stator columns s + b * 32 to s + b * 32 + 31, taken modulo 128, for every b.
All inputs are finite; a program needn't handle non-finite values.
Results may differ from a plain program's by a relative error of at most 0.0001.
Values sent between devices are 32-bit elements; how exact they have to be, the bound alone decides.
A program may use at most 64 MiB of HBM per device.

v0:
```python
import functools

import jax
import jax.numpy as jnp
from jax import lax
from jax.experimental import pallas as pl
from jax.experimental.pallas import tpu as pltpu
from jax.sharding import PartitionSpec as P

MESH = pl.DeviceIdType.MESH
PAD = 8
GROUP = 8


def total(terms):
    while len(terms) > 1:
        pairs = [a + b for a, b in zip(terms[::2], terms[1::2])]
        if len(terms) % 2:
            pairs.append(terms[-1])
        terms = pairs
    return terms[0]


def kernel(
    sectors, slabs,
    state, source, inverse, axial_in, cross_in, owner_in,
    res_out, state_out,
    axial, cross, owner, picks_wide, picks,
    q, src, inv, eff, prov, upd, facing, entering, following,
    local_sem, ax_send, ax_recv, se_send, se_recv,
    if_send, if_recv, fw_send, fw_recv, bw_send, bw_recv,
):
    nv, planes, columns, cells = src.shape
    groups = columns // GROUP
    row = lax.axis_index("row")
    sector = lax.axis_index("sector")
    slab = lax.axis_index("slab")
    has_low = slab > 0
    has_high = slab < slabs - 1
    rotor_top = jnp.logical_and(row == 0, slab == slabs - 1)
    stator_foot = jnp.logical_and(row == 1, slab == 0)
    on_plane = jnp.logical_or(rotor_top, stator_foot)
    after = lax.rem(sector + 1, sectors)
    before = lax.rem(sector + sectors - 1, sectors)
    facing_slab = jnp.where(row == 0, 0, slabs - 1)
    body = pl.ds(PAD, columns)

    load_state = pltpu.make_async_copy(
        state.at[0], q.at[:, pl.ds(1, planes), body], local_sem.at[0]
    )
    load_state.start()
    load_owner = pltpu.make_async_copy(owner_in, owner, local_sem.at[3])
    load_owner.start()
    load_axial = pltpu.make_async_copy(axial_in, axial, local_sem.at[4])
    load_axial.start()
    load_cross = pltpu.make_async_copy(cross_in, cross, local_sem.at[5])
    load_cross.start()
    load_inverse = pltpu.make_async_copy(inverse.at[0], inv, local_sem.at[2])
    load_inverse.start()
    load_source = pltpu.make_async_copy(source.at[0], src, local_sem.at[1])
    load_source.start()

    barrier = pltpu.get_barrier_semaphore()

    def greet(**where):
        pl.semaphore_signal(barrier, inc=1, device_id=where, device_id_type=MESH)

    @pl.when(on_plane)
    def _():
        for other in range(sectors):
            greet(row=1 - row, sector=other, slab=facing_slab)

    greet(sector=after)
    greet(sector=before)

    @pl.when(has_low)
    def _():
        greet(slab=slab - 1)

    @pl.when(has_high)
    def _():
        greet(slab=slab + 1)

    zero_plane = jnp.zeros((nv, columns, cells), jnp.float32)

    @pl.when(jnp.logical_not(has_low))
    def _():
        q[:, 0, body] = zero_plane

    @pl.when(jnp.logical_not(has_high))
    def _():
        q[:, planes + 1, body] = zero_plane

    load_owner.wait()
    shape = (columns, owner.shape[1])
    ids = sector * columns + lax.broadcasted_iota(jnp.int32, shape, 0)
    everyone = lax.broadcasted_iota(jnp.int32, shape, 1)
    owners = jnp.broadcast_to(owner[...], shape)
    is_rotor = jnp.broadcast_to(row, shape) == 0
    hits = jnp.where(is_rotor, everyone, owners) == ids
    found = jnp.sum(
        jnp.where(hits, jnp.where(is_rotor, owners, everyone), 0), axis=1, keepdims=True
    )
    found = jnp.minimum(found, owner.shape[1] - 1)
    picks_wide[...] = jnp.broadcast_to(found, picks_wide.shape)
    move_picks = pltpu.make_async_copy(picks_wide, picks, local_sem.at[6])
    move_picks.start()
    peers = 2 + has_low.astype(jnp.int32) + has_high.astype(jnp.int32)
    pl.semaphore_wait(barrier, peers + jnp.where(on_plane, sectors, 0))

    load_state.wait()

    def remote(source_ref, target_ref, send, recv, **where):
        return pltpu.make_async_remote_copy(
            src_ref=source_ref, dst_ref=target_ref, send_sem=send, recv_sem=recv,
            device_id=where, device_id_type=MESH,
        )

    def facing_copy(plane_at, other):
        return remote(
            q.at[:, plane_at, body], facing.at[sector], if_send.at[other], if_recv.at[sector],
            row=1 - row, sector=other, slab=facing_slab,
        )

    def facing_arrival(other):
        return remote(
            q.at[:, 1, body], facing.at[other], if_send.at[other], if_recv.at[other],
            row=1 - row, sector=other, slab=facing_slab,
        )

    @pl.when(rotor_top)
    def _():
        for other in range(sectors):
            facing_copy(planes, other).start()

    @pl.when(stator_foot)
    def _():
        for other in range(sectors):
            facing_copy(1, other).start()

    inner = pl.ds(1, planes)
    to_after = remote(
        q.at[:, inner, pl.ds(PAD + columns - 1, 1)], q.at[:, inner, pl.ds(PAD - 1, 1)],
        se_send.at[0], se_recv.at[0], sector=after,
    )
    to_before = remote(
        q.at[:, inner, pl.ds(PAD, 1)], q.at[:, inner, pl.ds(PAD + columns, 1)],
        se_send.at[1], se_recv.at[1], sector=before,
    )
    to_after.start()
    to_before.start()
    to_high = remote(
        q.at[:, planes, body], q.at[:, 0, body], ax_send.at[0], ax_recv.at[0], slab=slab + 1
    )
    to_low = remote(
        q.at[:, 1, body], q.at[:, planes + 1, body], ax_send.at[1], ax_recv.at[1], slab=slab - 1
    )

    @pl.when(has_high)
    def _():
        to_high.start()

    @pl.when(has_low)
    def _():
        to_low.start()

    load_inverse.wait()
    load_axial.wait()
    load_cross.wait()
    move_picks.wait()

    def effective(x, carry):
        for i in range(nv):
            blocks = [inv[i, j, x] for j in range(nv)]
            for k in range(nv):
                eff[i, k, x] = total([blocks[j] * (0.5 * axial[j, 0, k]) for j in range(nv)])
        return carry

    lax.fori_loop(0, planes, effective, 0)
    load_source.wait()
    to_after.wait_recv()
    to_before.wait_recv()

    @pl.when(has_high)
    def _():
        to_low.wait_recv()

    @pl.when(has_low)
    def _():
        to_high.wait_recv()

    def gather_facing(target):
        for other in range(sectors):
            facing_arrival(other).wait_recv()

        def pick(c, carry):
            at = picks[c, 0]
            part, column = at // columns, lax.rem(at, columns)
            for v in range(nv):
                target[v, pl.ds(c, 1)] = facing[part, v, pl.ds(column, 1)]
            return carry

        lax.fori_loop(0, columns, pick, 0)

    @pl.when(rotor_top)
    def _():
        gather_facing(q.at[:, planes + 1, body])

    lane = lax.broadcasted_iota(jnp.int32, (columns, cells), 1)

    def flux(x, carry):
        sums = [None] * nv
        for v in range(nv):
            here = q[v, x + 1, body]
            spans = (
                q[v, x + 2, body] - q[v, x, body],
                q[v, x + 1, pl.ds(PAD + 1, columns)] - q[v, x + 1, pl.ds(PAD - 1, columns)],
                jnp.where(lane == cells - 1, 0.0, pltpu.roll(here, cells - 1, 1))
                - jnp.where(lane == 0, 0.0, pltpu.roll(here, 1, 1)),
            )
            for i in range(nv):
                factors = (axial[i, 0, v], cross[0, i, 0, v], cross[0, i, 1, v])
                term = total([(0.5 * f) * s for f, s in zip(factors, spans)])
                sums[i] = term if sums[i] is None else sums[i] + term
        values = [src[i, x] - sums[i] for i in range(nv)]
        for i in range(nv):
            res_out[0, i, x] = values[i]
        for i in range(nv):
            prov[i, x] = total([inv[i, j, x] * values[j] for j in range(nv)])
        return carry

    lax.fori_loop(0, planes, flux, 0)

    @pl.when(jnp.logical_not(has_low))
    def _():
        entering[...] = zero_plane

    @pl.when(jnp.logical_not(has_high))
    def _():
        following[...] = zero_plane

    @pl.when(stator_foot)
    def _():
        gather_facing(entering)

    def columns_of(k):
        return pl.ds(pl.multiple_of(k * GROUP, GROUP), GROUP)

    def forward_copy(k):
        return remote(
            prov.at[:, planes - 1, columns_of(k)], entering.at[:, columns_of(k)],
            fw_send.at[k], fw_recv.at[k], slab=slab + 1,
        )

    def backward_copy(k):
        return remote(
            upd.at[:, 0, columns_of(k)], following.at[:, columns_of(k)],
            bw_send.at[k], bw_recv.at[k], slab=slab - 1,
        )

    def forward(k, carry):
        @pl.when(has_low)
        def _():
            forward_copy(k).wait_recv()

        at = columns_of(k)
        now = [entering[v, at] for v in range(nv)]
        for x in range(planes):
            now = [
                total([prov[i, x, at]] + [eff[i, j, x, at] * now[j] for j in range(nv)])
                for i in range(nv)
            ]
            for i in range(nv):
                prov[i, x, at] = now[i]

        @pl.when(has_high)
        def _():
            forward_copy(k).start()

        return carry

    lax.fori_loop(0, groups, forward, 0)

    @pl.when(stator_foot)
    def _():
        ghost = [entering[v] for v in range(nv)]
        for i in range(nv):
            res_out[0, i, 0] = res_out[0, i, 0] + total(
                [(0.5 * axial[i, 0, j]) * ghost[j] for j in range(nv)]
            )

    def backward(k, carry):
        @pl.when(has_high)
        def _():
            backward_copy(k).wait_recv()

        at = columns_of(k)
        shifted = pl.ds(pl.multiple_of(PAD + k * GROUP, GROUP), GROUP)
        now = [following[v, at] for v in range(nv)]
        for x in reversed(range(planes)):
            now = [
                prov[i, x, at] - total([eff[i, j, x, at] * now[j] for j in range(nv)])
                for i in range(nv)
            ]
            if x == 0:
                for i in range(nv):
                    upd[i, 0, at] = now[i]

                @pl.when(has_low)
                def _():
                    backward_copy(k).start()

            for i in range(nv):
                state_out[0, i, x, at] = q[i, x + 1, shifted] + now[i]
        return carry

    to_after.wait_send()
    to_before.wait_send()

    @pl.when(has_high)
    def _():
        to_high.wait_send()

    @pl.when(has_low)
    def _():
        to_low.wait_send()

    @pl.when(on_plane)
    def _():
        for other in range(sectors):
            facing_copy(1, other).wait_send()

    lax.fori_loop(0, groups, backward, 0)

    def finish(k, carry):
        @pl.when(has_high)
        def _():
            forward_copy(k).wait_send()

        @pl.when(has_low)
        def _():
            backward_copy(k).wait_send()

        return carry

    lax.fori_loop(0, groups, finish, 0)


def per_device(state, source, diag_inverse, jac_axial, jac_cross, owner):
    _, nv, planes, columns, cells = state.shape
    sectors = lax.axis_size("sector")
    slabs = lax.axis_size("slab")
    groups = columns // GROUP
    def vmem(*shape):
        return pltpu.VMEM(shape, jnp.float32)

    dma = pltpu.SemaphoreType.DMA
    field = (nv, planes, columns, cells)
    plane = (nv, columns, cells)
    anywhere = pl.BlockSpec(memory_space=pl.ANY)
    outside = pl.BlockSpec(memory_space=pltpu.HBM)
    return pl.pallas_call(
        functools.partial(kernel, sectors, slabs),
        out_shape=[vmem(*state.shape)] * 2,
        in_specs=[outside] * 6,
        out_specs=[pl.BlockSpec(memory_space=pltpu.VMEM)] * 2,
        scratch_shapes=[
            pltpu.SMEM((nv, 1, nv), jnp.float32),
            pltpu.SMEM((1, nv, 2, nv), jnp.float32),
            pltpu.VMEM((1, owner.shape[0]), jnp.int32),
            pltpu.VMEM((columns, 128), jnp.int32),
            pltpu.SMEM((columns, 128), jnp.int32),
            vmem(nv, planes + 2, columns + 2 * PAD, cells),
            vmem(*field),
            vmem(nv, *field),
            vmem(nv, *field),
            vmem(*field),
            vmem(nv, 1, columns, cells),
            vmem(sectors, *plane),
            vmem(*plane),
            vmem(*plane),
            dma((7,)),
            dma((2,)), dma((2,)), dma((2,)), dma((2,)),
            dma((sectors,)), dma((sectors,)),
            dma((groups,)), dma((groups,)), dma((groups,)), dma((groups,)),
        ],
        compiler_params=pltpu.CompilerParams(collective_id=0, has_side_effects=True),
    )(state, source, diag_inverse, jnp.swapaxes(jac_axial, 0, 1),
        jnp.swapaxes(jac_cross, 1, 2), owner[None])


def solution(mesh):
    return jax.shard_map(
        per_device,
        mesh=mesh,
        in_specs=(
            P("row", None, "slab", "sector", None),
            P("row", None, "slab", "sector", None),
            P("row", None, None, "slab", "sector", None),
            P("row", None, None),
            P("row", None, None, None),
            P(),
        ),
        out_specs=(P("row", None, "slab", "sector", None), P("row", None, "slab", "sector", None)),
        check_vma=False,
    )
```

profile of v0, /device:TPU:0, one launch (start us, length us, event | category | flops | bytes accessed | tf_op | source)
XLA Modules:
  0.0 35.4 jit_solution(15772680711455237516)
XLA Ops:
  0.6 33.1 %shard_map.77 = (f32[1,5,8,32,128]{4,3,2,1,0:T(8,128)S(1)}, f32[1,5,8,32,128]{4,3,2,1,0:T(8,128)S(1)}) custom-call(f32[1,5,8,32,128]{4,3,2,1,0:T(8,128)} %state.1, f32[1,5,8,32,128]{4,3,2,1,0:T(8,128)} %source.1, f32[1,5,5,8,32,128]{5,4,3,2,1,0:T(8,128)} %inverse.1, f32[5,1,5]{2,1,0:T(1,128)} %bitcast.4, f32[1,5,2,5]{3,2,1,0:T(2,128)} %bitcast.3, ...), custom_call_target="tpu_custom_call" | custom-call | tf_op jit(solution)/shard_map/pallas_call | solution.py:362
  33.7 0.8 %copy.10 = f32[1,5,8,32,128]{4,3,2,1,0:T(8,128)} copy(f32[1,5,8,32,128]{4,3,2,1,0:T(8,128)S(1)} %get-tuple-element.2) | data formatting | bytes 1310720
  34.5 0.8 %copy.11 = f32[1,5,8,32,128]{4,3,2,1,0:T(8,128)} copy(f32[1,5,8,32,128]{4,3,2,1,0:T(8,128)S(1)} %get-tuple-element.3) | data formatting | bytes 1310720
where the time goes:
time: 35.5 us; the launch traced here: 35.4 us
  Pallas kernels  33.1 us (93%)
  local copies, waits for them, and re-layouts  1.67 us (5%)
  between operations  0.64 us (2%)
    pallas_call x1, Pallas kernels, per_device(): pl.pallas_call(functools.partial(kernel, sectors, slabs), out_shape=[vmem...  33.1 us
    unnamed x2, local copies, waits for them, and re-layouts  1.67 us

commit v1 on v0

v1 whole, which is shorter than its diff:
```python
import functools

import jax
import jax.numpy as jnp
from jax import lax
from jax.experimental import pallas as pl
from jax.experimental.pallas import tpu as pltpu
from jax.sharding import PartitionSpec as P

MESH = pl.DeviceIdType.MESH
PAD = 8
GROUP = 8


def total(terms):
    while len(terms) > 1:
        pairs = [a + b for a, b in zip(terms[::2], terms[1::2])]
        if len(terms) % 2:
            pairs.append(terms[-1])
        terms = pairs
    return terms[0]


def both(*conditions):
    return functools.reduce(jnp.logical_and, conditions)


def kernel(
    sectors, slabs,
    state, source, inverse, axial_in, cross_in, owner_in,
    res_out, state_out,
    axial, cross, owner, picks_wide, picks,
    q, src, inv, eff, prov, below, above, facing, entering, following, leaving, upd,
    local_sem, ax_send, ax_recv, se_send, se_recv,
    if_send, if_recv, fw_send, fw_recv, bw_send, bw_recv, sectors_in,
):
    nv, planes, columns, cells = src.shape
    groups = columns // GROUP
    row = lax.axis_index("row")
    sector = lax.axis_index("sector")
    slab = lax.axis_index("slab")
    rotor, stator = row == 0, row == 1
    has_low = slab > 0
    has_high = slab < slabs - 1
    is_first, is_last = slab == 0, slab == slabs - 1
    middle = both(has_low, has_high)
    outer = jnp.logical_or(is_first, is_last)
    rotor_top = both(rotor, is_last)
    stator_foot = both(stator, is_first)
    on_plane = jnp.logical_or(rotor_top, stator_foot)
    after = lax.rem(sector + 1, sectors)
    before = lax.rem(sector + sectors - 1, sectors)
    facing_slab = jnp.where(row == 0, 0, slabs - 1)
    body = pl.ds(PAD, columns)

    load_state = pltpu.make_async_copy(state.at[0], q.at[:, :, body], local_sem.at[0])
    load_state.start()
    load_axial = pltpu.make_async_copy(axial_in, axial, local_sem.at[4])
    load_axial.start()
    load_inverse = pltpu.make_async_copy(inverse.at[0], inv, local_sem.at[2])
    load_inverse.start()
    load_cross = pltpu.make_async_copy(cross_in, cross, local_sem.at[5])
    load_cross.start()
    load_owner = pltpu.make_async_copy(owner_in, owner, local_sem.at[3])
    load_owner.start()
    load_source = pltpu.make_async_copy(source.at[0], src, local_sem.at[1])
    load_source.start()

    barrier = pltpu.get_barrier_semaphore()

    def greet(**where):
        pl.semaphore_signal(barrier, inc=1, device_id=where, device_id_type=MESH)

    @pl.when(on_plane)
    def _():
        for other in range(sectors):
            greet(row=1 - row, sector=other, slab=facing_slab)

    @pl.when(has_high)
    def _():
        greet(slab=slab + 1)

    @pl.when(jnp.logical_or(stator, outer))
    def _():
        greet(sector=after)
        greet(sector=before)

    @pl.when(both(rotor, middle))
    def _():
        greet(row=1, sector=after)
        greet(row=1, sector=before)
        greet(row=1)

    peers = (
        has_low.astype(jnp.int32)
        + jnp.where(jnp.logical_or(stator, outer), 2, 0)
        + jnp.where(both(stator, middle), 3, 0)
        + jnp.where(on_plane, sectors, 0)
    )

    zero_plane = jnp.zeros((nv, columns, cells), jnp.float32)

    @pl.when(is_first)
    def _():
        entering[...] = zero_plane
        below[...] = zero_plane

    @pl.when(is_last)
    def _():
        following[...] = zero_plane
        above[...] = zero_plane

    move_picks = pltpu.make_async_copy(picks_wide, picks, local_sem.at[6])
    load_owner.wait()

    @pl.when(on_plane)
    def _():
        shape = (columns, owner.shape[1])
        ids = sector * columns + lax.broadcasted_iota(jnp.int32, shape, 0)
        everyone = lax.broadcasted_iota(jnp.int32, shape, 1)
        owners = jnp.broadcast_to(owner[...], shape)
        is_rotor = jnp.broadcast_to(row, shape) == 0
        hits = jnp.where(is_rotor, everyone, owners) == ids
        found = jnp.sum(
            jnp.where(hits, jnp.where(is_rotor, owners, everyone), 0), axis=1, keepdims=True
        )
        found = jnp.minimum(found, owner.shape[1] - 1)
        picks_wide[...] = jnp.broadcast_to(found, picks_wide.shape)
        move_picks.start()

    def remote(source_ref, target_ref, send, recv, **where):
        return pltpu.make_async_remote_copy(
            src_ref=source_ref, dst_ref=target_ref, send_sem=send, recv_sem=recv,
            device_id=where, device_id_type=MESH,
        )

    def facing_copy(plane_at, other):
        return remote(
            q.at[:, plane_at, body], facing.at[sector], if_send.at[other], if_recv.at[sector],
            row=1 - row, sector=other, slab=facing_slab,
        )

    def facing_arrival(other):
        return remote(
            q.at[:, 0, body], facing.at[other], if_send.at[other], if_recv.at[other],
            row=1 - row, sector=other, slab=facing_slab,
        )

    to_after = remote(
        q.at[:, :, pl.ds(PAD + columns - 1, 1)], q.at[:, :, pl.ds(PAD - 1, 1)],
        se_send.at[0], se_recv.at[0], sector=after,
    )
    to_before = remote(
        q.at[:, :, pl.ds(PAD, 1)], q.at[:, :, pl.ds(PAD + columns, 1)],
        se_send.at[1], se_recv.at[1], sector=before,
    )
    to_high = remote(
        q.at[:, planes - 1, body], below, ax_send.at[0], ax_recv.at[0], slab=slab + 1
    )
    to_low = remote(
        q.at[:, 0, body], above, ax_send.at[1], ax_recv.at[1], slab=slab - 1
    )

    def open_up():
        pl.semaphore_wait(barrier, peers)
        load_state.wait()

        @pl.when(has_low)
        def _():
            to_low.start()

        @pl.when(rotor_top)
        def _():
            for other in range(sectors):
                facing_copy(planes - 1, other).start()

        @pl.when(stator_foot)
        def _():
            for other in range(sectors):
                facing_copy(0, other).start()

        @pl.when(both(stator, middle))
        def _():
            pl.semaphore_signal(
                sectors_in, inc=1, device_id=dict(row=0), device_id_type=MESH
            )

    def products():
        load_axial.wait()
        load_inverse.wait()

        def effective(x, carry):
            for i in range(nv):
                blocks = [inv[i, j, x] for j in range(nv)]
                for k in range(nv):
                    eff[i, k, x] = total([blocks[j] * (0.5 * axial[j, 0, k]) for j in range(nv)])
            return carry

        lax.fori_loop(0, planes, effective, 0)

    far = sector >= sectors // 2
    early = both(rotor, jnp.logical_or(middle, both(is_last, far)))
    opens_at = jnp.where(early, 0, 2)

    def prepare(step, carry):
        pl.when(step == opens_at)(open_up)
        pl.when(step == 1)(products)
        return carry

    lax.fori_loop(0, 3, prepare, 0)

    @pl.when(both(rotor, middle))
    def _():
        pl.semaphore_wait(sectors_in, 1)

    to_after.start()
    to_before.start()
    load_cross.wait()
    load_source.wait()

    def columns_of(g):
        return pl.ds(pl.multiple_of(g * GROUP, GROUP), GROUP)

    def padded(g, shift=0):
        if shift:
            return pl.ds(PAD + g * GROUP + shift, GROUP)
        return pl.ds(pl.multiple_of(PAD + g * GROUP, GROUP), GROUP)

    lane = lax.broadcasted_iota(jnp.int32, (GROUP, cells), 1)
    no_cells = jnp.zeros((GROUP, cells), jnp.float32)

    def flux(g):
        at = columns_of(g)

        def one(x, carry):
            higher = jnp.minimum(x + 1, planes - 1)
            lower = jnp.maximum(x - 1, 0)
            sums = [None] * nv
            for v in range(nv):
                here = q[v, x, padded(g)]
                spans = (
                    jnp.where(x == planes - 1, no_cells, q[v, higher, padded(g)])
                    - jnp.where(x == 0, no_cells, q[v, lower, padded(g)]),
                    q[v, x, padded(g, 1)] - q[v, x, padded(g, -1)],
                    jnp.where(lane == cells - 1, 0.0, pltpu.roll(here, cells - 1, 1))
                    - jnp.where(lane == 0, 0.0, pltpu.roll(here, 1, 1)),
                )
                for i in range(nv):
                    factors = (axial[i, 0, v], cross[0, i, 0, v], cross[0, i, 1, v])
                    term = total([(0.5 * f) * s for f, s in zip(factors, spans)])
                    sums[i] = term if sums[i] is None else sums[i] + term
            values = [src[i, x, at] - sums[i] for i in range(nv)]
            for i in range(nv):
                res_out[0, i, x, at] = values[i]
            for i in range(nv):
                prov[i, x, at] = total([inv[i, j, x, at] * values[j] for j in range(nv)])
            return carry

        lax.fori_loop(0, planes, one, 0)

    def gather_facing(*targets):
        move_picks.wait()
        for other in range(sectors):
            facing_arrival(other).wait_recv()

        def pick(block, carry):
            for inner in range(GROUP):
                c = block * GROUP + inner
                at = picks[c, 0]
                part, column = at // columns, lax.rem(at, columns)
                for v in range(nv):
                    value = facing[part, v, pl.ds(column, 1)]
                    for target in targets:
                        target[v, pl.ds(c, 1)] = value
            return carry

        lax.fori_loop(0, groups, pick, 0)

    def forward_copy(g):
        return remote(
            leaving.at[:, columns_of(g)], entering.at[:, columns_of(g)],
            fw_send.at[g], fw_recv.at[g], slab=slab + 1,
        )

    def backward_copy(g):
        return remote(
            upd.at[:, columns_of(g)], following.at[:, columns_of(g)],
            bw_send.at[g], bw_recv.at[g], slab=slab - 1,
        )

    def sweep_up(g):
        at = columns_of(g)
        now = [entering[v, at] for v in range(nv)]
        for x in range(planes):
            if x == planes - 1:
                now = [now[v] - above[v, at] for v in range(nv)]
            now = [
                total([prov[i, x, at]] + [eff[i, j, x, at] * now[j] for j in range(nv)])
                for i in range(nv)
            ]
            for i in range(nv):
                prov[i, x, at] = now[i]

        @pl.when(has_high)
        def _():
            for i in range(nv):
                leaving[i, at] = now[i] + q[i, planes - 1, padded(g)]
            forward_copy(g).start()

    def sweep_down(g):
        at = columns_of(g)
        now = [following[v, at] for v in range(nv)]
        for x in reversed(range(planes)):
            now = [
                prov[i, x, at] - total([eff[i, j, x, at] * now[j] for j in range(nv)])
                for i in range(nv)
            ]
            if x == 0:
                for i in range(nv):
                    upd[i, at] = now[i]

                @pl.when(has_low)
                def _():
                    backward_copy(g).start()

            for i in range(nv):
                state_out[0, i, x, at] = q[i, x, padded(g)] + now[i]

    leads = both(rotor, is_first)
    inside = groups - 2

    def advance(step, carry):
        late = step >= 2 * inside
        fluxes = jnp.where(
            leads,
            jnp.logical_or(step < inside, both(late, lax.rem(step, 2) == 0)),
            step < groups,
        )
        flux_at = jnp.where(jnp.logical_and(leads, late), step // 2, step)
        sweep_at = jnp.where(
            leads, jnp.where(late, step // 2, step - inside), step - groups
        )

        @pl.when(fluxes)
        def _():
            @pl.when(flux_at == inside)
            def _():
                to_before.wait_recv()

            @pl.when(flux_at == inside + 1)
            def _():
                to_after.wait_recv()

            flux(lax.rem(flux_at + 1, groups))

        @pl.when(jnp.logical_not(fluxes))
        def _():
            g = lax.rem(sweep_at + 1, groups)

            @pl.when(sweep_at == 0)
            def _():
                @pl.when(has_high)
                def _():
                    to_low.wait_recv()
                    to_high.start()

                pl.when(rotor_top)(functools.partial(gather_facing, above))
                pl.when(stator_foot)(functools.partial(gather_facing, entering, below))

            @pl.when(has_low)
            def _():
                forward_copy(g).wait_recv()

            sweep_up(g)

            @pl.when(is_last)
            def _():
                sweep_down(g)

        return carry

    lax.fori_loop(0, 2 * groups, advance, 0)

    @pl.when(has_low)
    def _():
        to_high.wait_recv()

    for i in range(nv):
        res_out[0, i, 0] = res_out[0, i, 0] + total(
            [(0.5 * axial[i, 0, j]) * below[j] for j in range(nv)]
        )
    for i in range(nv):
        res_out[0, i, planes - 1] = res_out[0, i, planes - 1] - total(
            [(0.5 * axial[i, 0, j]) * above[j] for j in range(nv)]
        )

    to_after.wait_send()
    to_before.wait_send()

    @pl.when(has_high)
    def _():
        to_high.wait_send()

    @pl.when(has_low)
    def _():
        to_low.wait_send()

    @pl.when(on_plane)
    def _():
        for other in range(sectors):
            facing_copy(0, other).wait_send()

    @pl.when(has_high)
    def _():
        def back(step, carry):
            g = lax.rem(step + 1, groups)
            backward_copy(g).wait_recv()
            sweep_down(g)
            return carry

        lax.fori_loop(0, groups, back, 0)

    def finish(g, carry):
        @pl.when(has_high)
        def _():
            forward_copy(g).wait_send()

        @pl.when(has_low)
        def _():
            backward_copy(g).wait_send()

        return carry

    lax.fori_loop(0, groups, finish, 0)


def write_out(res_in, state_in, res_out, state_out, sems):
    first = pltpu.make_async_copy(res_in, res_out, sems.at[0])
    second = pltpu.make_async_copy(state_in, state_out, sems.at[1])
    first.start()
    second.start()
    first.wait()
    second.wait()


def per_device(state, source, diag_inverse, jac_axial, jac_cross, owner):
    _, nv, planes, columns, cells = state.shape
    sectors = lax.axis_size("sector")
    slabs = lax.axis_size("slab")
    groups = columns // GROUP

    def vmem(*shape):
        return pltpu.VMEM(shape, jnp.float32)

    dma = pltpu.SemaphoreType.DMA
    field = (nv, planes, columns, cells)
    plane = (nv, columns, cells)
    outside = pl.BlockSpec(memory_space=pltpu.HBM)
    inside = pl.BlockSpec(memory_space=pltpu.VMEM)
    residual, new_state = pl.pallas_call(
        functools.partial(kernel, sectors, slabs),
        out_shape=[vmem(*state.shape)] * 2,
        in_specs=[outside] * 6,
        out_specs=[inside] * 2,
        scratch_shapes=[
            pltpu.SMEM((nv, 1, nv), jnp.float32),
            pltpu.SMEM((1, nv, 2, nv), jnp.float32),
            pltpu.VMEM((1, owner.shape[0]), jnp.int32),
            pltpu.VMEM((columns, 128), jnp.int32),
            pltpu.SMEM((columns, 128), jnp.int32),
            vmem(nv, planes, columns + 2 * PAD, cells),
            vmem(*field),
            vmem(nv, *field),
            vmem(nv, *field),
            vmem(*field),
            vmem(*plane),
            vmem(*plane),
            vmem(sectors, *plane),
            vmem(*plane),
            vmem(*plane),
            vmem(*plane),
            vmem(*plane),
            dma((7,)),
            dma((2,)), dma((2,)), dma((2,)), dma((2,)),
            dma((sectors,)), dma((sectors,)),
            dma((groups,)), dma((groups,)), dma((groups,)), dma((groups,)),
            pltpu.SemaphoreType.REGULAR,
        ],
        compiler_params=pltpu.CompilerParams(collective_id=0, has_side_effects=True),
    )(state, source, diag_inverse, jnp.swapaxes(jac_axial, 0, 1),
        jnp.swapaxes(jac_cross, 1, 2), owner[None])
    return pl.pallas_call(
        write_out,
        out_shape=[jax.ShapeDtypeStruct(state.shape, jnp.float32)] * 2,
        in_specs=[inside] * 2,
        out_specs=[outside] * 2,
        scratch_shapes=[dma((2,))],
        compiler_params=pltpu.CompilerParams(vmem_limit_bytes=1 << 20),
    )(
        pltpu.with_memory_space_constraint(residual, pltpu.VMEM),
        pltpu.with_memory_space_constraint(new_state, pltpu.VMEM),
    )


def solution(mesh):
    return jax.shard_map(
        per_device,
        mesh=mesh,
        in_specs=(
            P("row", None, "slab", "sector", None),
            P("row", None, "slab", "sector", None),
            P("row", None, None, "slab", "sector", None),
            P("row", None, None),
            P("row", None, None, None),
            P(),
        ),
        out_specs=(P("row", None, "slab", "sector", None), P("row", None, "slab", "sector", None)),
        check_vma=False,
    )
```

time: 35.5 us -> 33 us (0.930)
  local copies, waits for them, and re-layouts: 1.67 us -> 0 us
  Pallas kernels: 33.1 us -> 32.2 us
    pallas_call x1, Pallas kernels: 33.1 us -> 31.1 us  [per_device(): pl.pallas_call(functools.partial(kernel, sectors, slabs), out_shape=[vmem...]
    unnamed x2 -> x0, local copies, waits for them, and re-layouts: 1.67 us -> none
    pallas_call x0 -> x1, Pallas kernels: none -> 1.07 us  [per_device(): pl.pallas_call(write_out, out_shape=[jax.ShapeDtypeStruct(state.shape, jn...]
where the time goes in v1:
time: 33 us; the launch traced here: 32.9 us
  Pallas kernels  32.2 us (98%)
  between operations  0.64 us (2%)
    pallas_call x1, Pallas kernels, per_device(): pl.pallas_call(functools.partial(kernel, sectors, slabs), out_shape=[vmem...  31.1 us
    pallas_call x1, Pallas kernels, per_device(): pl.pallas_call(write_out, out_shape=[jax.ShapeDtypeStruct(state.shape, jn...  1.07 us

profile of v1, /device:TPU:0, one launch (start us, length us, event | category | flops | bytes accessed | tf_op | source)
XLA Modules:
  0.0 32.9 jit_solution(289386177088367292)
XLA Ops:
  0.6 31.1 %shard_map.77 = (f32[1,5,8,32,128]{4,3,2,1,0:T(8,128)S(1)}, f32[1,5,8,32,128]{4,3,2,1,0:T(8,128)S(1)}) custom-call(f32[1,5,8,32,128]{4,3,2,1,0:T(8,128)} %state.1, f32[1,5,8,32,128]{4,3,2,1,0:T(8,128)} %source.1, f32[1,5,5,8,32,128]{5,4,3,2,1,0:T(8,128)} %inverse.1, f32[5,1,5]{2,1,0:T(1,128)} %bitcast.4, f32[1,5,2,5]{3,2,1,0:T(2,128)} %bitcast.3, ...), custom_call_target="tpu_custom_call" | custom-call | tf_op jit(solution)/shard_map/pallas_call | solution.py:460
  31.8 1.1 %shard_map.78 = (f32[1,5,8,32,128]{4,3,2,1,0:T(8,128)}, f32[1,5,8,32,128]{4,3,2,1,0:T(8,128)}) custom-call(f32[1,5,8,32,128]{4,3,2,1,0:T(8,128)S(1)} %get-tuple-element.4.res_in, f32[1,5,8,32,128]{4,3,2,1,0:T(8,128)S(1)} %get-tuple-element.5.state_in), custom_call_target="tpu_custom_call" | custom-call | tf_op jit(solution)/shard_map/pallas_call | solution.py:492

commit v2 on v1

--- a/solution.py
+++ b/solution.py
@@ -30,7 +30,7 @@
     state, source, inverse, axial_in, cross_in, owner_in,
     res_out, state_out,
     axial, cross, owner, picks_wide, picks,
-    q, src, inv, eff, prov, below, above, facing, entering, following, leaving, upd,
+    q, halo, src, inv, eff, prov, below, above, facing, entering, following, leaving, upd,
     local_sem, ax_send, ax_recv, se_send, se_recv,
     if_send, if_recv, fw_send, fw_recv, bw_send, bw_recv, sectors_in,
 ):
@@ -99,6 +99,9 @@
     )
 
     zero_plane = jnp.zeros((nv, columns, cells), jnp.float32)
+    zero_columns = jnp.zeros((nv, planes, PAD, cells), jnp.float32)
+    q[:, :, pl.ds(0, PAD)] = zero_columns
+    q[:, :, pl.ds(PAD + columns, PAD)] = zero_columns
 
     @pl.when(is_first)
     def _():
@@ -147,13 +150,19 @@
         )
 
     to_after = remote(
-        q.at[:, :, pl.ds(PAD + columns - 1, 1)], q.at[:, :, pl.ds(PAD - 1, 1)],
+        q.at[:, :, pl.ds(PAD + columns - 1, 1)], halo.at[0],
         se_send.at[0], se_recv.at[0], sector=after,
     )
     to_before = remote(
-        q.at[:, :, pl.ds(PAD, 1)], q.at[:, :, pl.ds(PAD + columns, 1)],
+        q.at[:, :, pl.ds(PAD, 1)], halo.at[1],
         se_send.at[1], se_recv.at[1], sector=before,
     )
+
+    def halo_arrival(side):
+        return remote(
+            q.at[:, :, pl.ds(PAD, 1)], halo.at[side],
+            se_send.at[side], se_recv.at[side], sector=before,
+        )
     to_high = remote(
         q.at[:, planes - 1, body], below, ax_send.at[0], ax_recv.at[0], slab=slab + 1
     )
@@ -161,9 +170,10 @@
         q.at[:, 0, body], above, ax_send.at[1], ax_recv.at[1], slab=slab - 1
     )
 
+    at_start = sector == 0
+
     def open_up():
         pl.semaphore_wait(barrier, peers)
-        load_state.wait()
 
         @pl.when(has_low)
         def _():
@@ -185,75 +195,100 @@
                 sectors_in, inc=1, device_id=dict(row=0), device_id_type=MESH
             )
 
-    def products():
+    def meet_sectors():
+        @pl.when(both(rotor, middle))
+        def _():
+            pl.semaphore_wait(sectors_in, 1)
+
+        to_after.start()
+        to_before.start()
+
+    def columns_of(g):
+        return pl.ds(pl.multiple_of(g * GROUP, GROUP), GROUP)
+
+    def padded(g):
+        return pl.ds(pl.multiple_of(PAD + g * GROUP, GROUP), GROUP)
+
+    lane = lax.broadcasted_iota(jnp.int32, (columns, cells), 1)
+    no_cells = jnp.zeros((columns, cells), jnp.float32)
+
+    def effective(x, carry):
+        for i in range(nv):
+            blocks = [inv[i, j, x] for j in range(nv)]
+            for k in range(nv):
+                eff[i, k, x] = total([blocks[j] * (0.5 * axial[j, 0, k]) for j in range(nv)])
+        return carry
+
+    def flux(x, carry):
+        higher = jnp.minimum(x + 1, planes - 1)
+        lower = jnp.maximum(x - 1, 0)
+        sums = [None] * nv
+        for v in range(nv):
+            here = q[v, x, body]
+            spans = (
+                jnp.where(x == planes - 1, no_cells, q[v, higher, body])
+                - jnp.where(x == 0, no_cells, q[v, lower, body]),
+                q[v, x, pl.ds(PAD + 1, columns)] - q[v, x, pl.ds(PAD - 1, columns)],
+                jnp.where(lane == cells - 1, 0.0, pltpu.roll(here, cells - 1, 1))
+                - jnp.where(lane == 0, 0.0, pltpu.roll(here, 1, 1)),
+            )
+            for i in range(nv):
+                factors = (axial[i, 0, v], cross[0, i, 0, v], cross[0, i, 1, v])
+                term = total([f * s for f, s in zip(factors, spans)])
+                sums[i] = term if sums[i] is None else sums[i] + term
+        values = [src[i, x] - 0.5 * sums[i] for i in range(nv)]
+        for i in range(nv):
+            res_out[0, i, x] = values[i]
+        for i in range(nv):
+            prov[i, x] = total([inv[i, j, x] * values[j] for j in range(nv)])
+        return carry
+
+    def local_work():
         load_axial.wait()
         load_inverse.wait()
-
-        def effective(x, carry):
-            for i in range(nv):
-                blocks = [inv[i, j, x] for j in range(nv)]
-                for k in range(nv):
-                    eff[i, k, x] = total([blocks[j] * (0.5 * axial[j, 0, k]) for j in range(nv)])
-            return carry
-
         lax.fori_loop(0, planes, effective, 0)
-
-    far = sector >= sectors // 2
-    early = both(rotor, jnp.logical_or(middle, both(is_last, far)))
+        load_cross.wait()
+        load_source.wait()
+        lax.fori_loop(0, planes, flux, 0)
+
+    early = jnp.logical_or(jnp.logical_not(at_start), both(rotor, middle))
     opens_at = jnp.where(early, 0, 2)
+    meets_at = jnp.where(at_start, 2, 0)
+    load_state.wait()
 
     def prepare(step, carry):
         pl.when(step == opens_at)(open_up)
-        pl.when(step == 1)(products)
+        pl.when(step == meets_at)(meet_sectors)
+        pl.when(step == 1)(local_work)
         return carry
 
     lax.fori_loop(0, 3, prepare, 0)
-
-    @pl.when(both(rotor, middle))
-    def _():
-        pl.semaphore_wait(sectors_in, 1)
-
-    to_after.start()
-    to_before.start()
-    load_cross.wait()
-    load_source.wait()
-
-    def columns_of(g):
-        return pl.ds(pl.multiple_of(g * GROUP, GROUP), GROUP)
-
-    def padded(g, shift=0):
-        if shift:
-            return pl.ds(PAD + g * GROUP + shift, GROUP)
-        return pl.ds(pl.multiple_of(PAD + g * GROUP, GROUP), GROUP)
-
-    lane = lax.broadcasted_iota(jnp.int32, (GROUP, cells), 1)
-    no_cells = jnp.zeros((GROUP, cells), jnp.float32)
-
-    def flux(g):
-        at = columns_of(g)
+    place = lax.broadcasted_iota(jnp.int32, (GROUP, cells), 0)
+
+    def mend(side):
+        halo_arrival(side).wait_recv()
+        at = columns_of(side * (groups - 1))
+        touched = place == side * (GROUP - 1)
+        scale = jnp.where(side == 0, 0.5, -0.5)
 
         def one(x, carry):
-            higher = jnp.minimum(x + 1, planes - 1)
-            lower = jnp.maximum(x - 1, 0)
-            sums = [None] * nv
-            for v in range(nv):
-                here = q[v, x, padded(g)]
-                spans = (
-                    jnp.where(x == planes - 1, no_cells, q[v, higher, padded(g)])
-                    - jnp.where(x == 0, no_cells, q[v, lower, padded(g)]),
-                    q[v, x, padded(g, 1)] - q[v, x, padded(g, -1)],
-                    jnp.where(lane == cells - 1, 0.0, pltpu.roll(here, cells - 1, 1))
-                    - jnp.where(lane == 0, 0.0, pltpu.roll(here, 1, 1)),
+            outside = [
+                jnp.broadcast_to(halo[side, v, x], (GROUP, cells)) for v in range(nv)
+            ]
+            change = [
+                jnp.where(
+                    touched,
+                    scale * total([cross[0, i, 0, v] * outside[v] for v in range(nv)]),
+                    0.0,
                 )
-                for i in range(nv):
-                    factors = (axial[i, 0, v], cross[0, i, 0, v], cross[0, i, 1, v])
-                    term = total([(0.5 * f) * s for f, s in zip(factors, spans)])
-                    sums[i] = term if sums[i] is None else sums[i] + term
-            values = [src[i, x, at] - sums[i] for i in range(nv)]
+                for i in range(nv)
+            ]
             for i in range(nv):
-                res_out[0, i, x, at] = values[i]
+                res_out[0, i, x, at] = res_out[0, i, x, at] + change[i]
             for i in range(nv):
-                prov[i, x, at] = total([inv[i, j, x, at] * values[j] for j in range(nv)])
+                prov[i, x, at] = prov[i, x, at] + total(
+                    [inv[i, j, x, at] * change[j] for j in range(nv)]
+                )
             return carry
 
         lax.fori_loop(0, planes, one, 0)
@@ -326,34 +361,24 @@
             for i in range(nv):
                 state_out[0, i, x, at] = q[i, x, padded(g)] + now[i]
 
-    leads = both(rotor, is_first)
+    leads = both(rotor, slab <= 1)
     inside = groups - 2
 
     def advance(step, carry):
-        late = step >= 2 * inside
-        fluxes = jnp.where(
-            leads,
-            jnp.logical_or(step < inside, both(late, lax.rem(step, 2) == 0)),
-            step < groups,
-        )
-        flux_at = jnp.where(jnp.logical_and(leads, late), step // 2, step)
+        mends = jnp.where(
+            leads, jnp.logical_or(step == inside, step == groups), step < 2
+        )
+        side = jnp.where(step == jnp.where(leads, inside, 0), 1, 0)
         sweep_at = jnp.where(
-            leads, jnp.where(late, step // 2, step - inside), step - groups
-        )
-
-        @pl.when(fluxes)
-        def _():
-            @pl.when(flux_at == inside)
-            def _():
-                to_before.wait_recv()
-
-            @pl.when(flux_at == inside + 1)
-            def _():
-                to_after.wait_recv()
-
-            flux(lax.rem(flux_at + 1, groups))
-
-        @pl.when(jnp.logical_not(fluxes))
+            leads, step - (step > inside).astype(jnp.int32) - (step > groups).astype(jnp.int32),
+            step - 2,
+        )
+
+        @pl.when(mends)
+        def _():
+            mend(side)
+
+        @pl.when(jnp.logical_not(mends))
         def _():
             g = lax.rem(sweep_at + 1, groups)
 
@@ -379,7 +404,7 @@
 
         return carry
 
-    lax.fori_loop(0, 2 * groups, advance, 0)
+    lax.fori_loop(0, groups + 2, advance, 0)
 
     @pl.when(has_low)
     def _():
@@ -469,6 +494,7 @@
             pltpu.VMEM((columns, 128), jnp.int32),
             pltpu.SMEM((columns, 128), jnp.int32),
             vmem(nv, planes, columns + 2 * PAD, cells),
+            vmem(2, nv, planes, 1, cells),
             vmem(*field),
             vmem(nv, *field),
             vmem(nv, *field),

time: 33 us -> 33.1 us (level)
  no operation moved by 1% of the time
where the time goes in v2:
time: 33.1 us; the launch traced here: 32.9 us
  Pallas kernels  32.3 us (98%)
  between operations  0.64 us (2%)
    pallas_call x1, Pallas kernels, per_device(): pl.pallas_call(functools.partial(kernel, sectors, slabs), out_shape=[vmem...  31.2 us
    pallas_call x1, Pallas kernels, per_device(): pl.pallas_call(write_out, out_shape=[jax.ShapeDtypeStruct(state.shape, jn...  1.07 us

profile of v2, /device:TPU:0, one launch (start us, length us, event | category | flops | bytes accessed | tf_op | source)
XLA Modules:
  0.0 32.9 jit_solution(11330893237281428045)
XLA Ops:
  0.6 31.2 %shard_map.77 = (f32[1,5,8,32,128]{4,3,2,1,0:T(8,128)S(1)}, f32[1,5,8,32,128]{4,3,2,1,0:T(8,128)S(1)}) custom-call(f32[1,5,8,32,128]{4,3,2,1,0:T(8,128)} %state.1, f32[1,5,8,32,128]{4,3,2,1,0:T(8,128)} %source.1, f32[1,5,5,8,32,128]{5,4,3,2,1,0:T(8,128)} %inverse.1, f32[5,1,5]{2,1,0:T(1,128)} %bitcast.4, f32[1,5,2,5]{3,2,1,0:T(2,128)} %bitcast.3, ...), custom_call_target="tpu_custom_call" | custom-call | tf_op jit(solution)/shard_map/pallas_call | solution.py:485
  31.8 1.1 %shard_map.78 = (f32[1,5,8,32,128]{4,3,2,1,0:T(8,128)}, f32[1,5,8,32,128]{4,3,2,1,0:T(8,128)}) custom-call(f32[1,5,8,32,128]{4,3,2,1,0:T(8,128)S(1)} %get-tuple-element.4.res_in, f32[1,5,8,32,128]{4,3,2,1,0:T(8,128)S(1)} %get-tuple-element.5.state_in), custom_call_target="tpu_custom_call" | custom-call | tf_op jit(solution)/shard_map/pallas_call | solution.py:518

commit v3 on v2

--- a/solution.py
+++ b/solution.py
@@ -31,8 +31,10 @@
     res_out, state_out,
     axial, cross, owner, picks_wide, picks,
     q, halo, src, inv, eff, prov, below, above, facing, entering, following, leaving, upd,
+    base, mats_out, mats_in, powers, trial,
     local_sem, ax_send, ax_recv, se_send, se_recv,
-    if_send, if_recv, fw_send, fw_recv, bw_send, bw_recv, sectors_in,
+    if_send, if_recv, fw_send, fw_recv, bw_send, bw_recv,
+    skip_send, base_recv, mat_send, mat_recv, sectors_in,
 ):
     nv, planes, columns, cells = src.shape
     groups = columns // GROUP
@@ -43,6 +45,8 @@
     has_low = slab > 0
     has_high = slab < slabs - 1
     is_first, is_last = slab == 0, slab == slabs - 1
+    is_second, is_third = slab == 1, slab == 2
+    is_turn = slab == slabs - 2
     middle = both(has_low, has_high)
     outer = jnp.logical_or(is_first, is_last)
     rotor_top = both(rotor, is_last)
@@ -323,9 +327,95 @@
             bw_send.at[g], bw_recv.at[g], slab=slab - 1,
         )
 
-    def sweep_up(g):
+    def skip_copy(g):
+        return remote(
+            upd.at[:, columns_of(g)], following.at[:, columns_of(g)],
+            skip_send.at[g], bw_recv.at[g], slab=0,
+        )
+
+    def base_copy(g):
+        return remote(
+            upd.at[:, columns_of(g)], base.at[:, columns_of(g)],
+            bw_send.at[g], base_recv.at[g], slab=0,
+        )
+
+    def mat_copy(g):
+        return remote(
+            mats_out.at[:, :, columns_of(g)], mats_in.at[:, :, columns_of(g)],
+            mat_send.at[g], mat_recv.at[g], slab=slab - 1,
+        )
+
+    def blocks_at(x, at):
+        return [[eff[i, j, x, at] for j in range(nv)] for i in range(nv)]
+
+    def times(left, right):
+        return [
+            [total([left[i][j] * right[j][k] for j in range(nv)]) for k in range(nv)]
+            for i in range(nv)
+        ]
+
+    def pack(matrix):
+        return tuple(matrix[i][k] for i in range(nv) for k in range(nv))
+
+    def unpack(values):
+        return [list(values[i * nv : i * nv + nv]) for i in range(nv)]
+
+    def send_matrix(g, values):
         at = columns_of(g)
-        now = [entering[v, at] for v in range(nv)]
+        matrix = unpack(values)
+        for i in range(nv):
+            for k in range(nv):
+                mats_out[i, k, at] = matrix[i][k]
+        mat_copy(g).start()
+
+    def entry_to_update(step, carry):
+        g = lax.rem(step + 1, groups)
+        at = columns_of(g)
+        first = blocks_at(0, at)
+        for i in range(nv):
+            for k in range(nv):
+                powers[i, k, 0] = first[i][k]
+
+        def up(x, values):
+            product = times(blocks_at(x, at), unpack(values))
+            for i in range(nv):
+                for k in range(nv):
+                    powers[i, k, x] = product[i][k]
+            return pack(product)
+
+        def down(step, values):
+            x = planes - 2 - step
+            product = times(blocks_at(x, at), unpack(values))
+            return pack(
+                [[powers[i, k, x] - product[i][k] for k in range(nv)] for i in range(nv)]
+            )
+
+        values = lax.fori_loop(1, planes, up, pack(first))
+        send_matrix(g, lax.fori_loop(0, planes - 1, down, values))
+        return carry
+
+    def exit_to_update(step, carry):
+        g = lax.rem(step + 1, groups)
+        at = columns_of(g)
+
+        def down(step, values):
+            product = times(blocks_at(planes - 2 - step, at), unpack(values))
+            return pack([[-value for value in line] for line in product])
+
+        last = [[-value for value in line] for line in blocks_at(planes - 1, at)]
+        send_matrix(g, lax.fori_loop(0, planes - 1, down, pack(last)))
+        return carry
+
+    @pl.when(is_last)
+    def _():
+        lax.fori_loop(0, groups, entry_to_update, 0)
+
+    @pl.when(is_second)
+    def _():
+        lax.fori_loop(0, groups, exit_to_update, 0)
+
+    def climb(g, now, keep):
+        at = columns_of(g)
         for x in range(planes):
             if x == planes - 1:
                 now = [now[v] - above[v, at] for v in range(nv)]
@@ -334,7 +424,16 @@
                 for i in range(nv)
             ]
             for i in range(nv):
-                prov[i, x, at] = now[i]
+                keep(i, x, now[i])
+        return now
+
+    def sweep_up(g):
+        at = columns_of(g)
+
+        def keep(i, x, value):
+            prov[i, x, at] = value
+
+        now = climb(g, [entering[v, at] for v in range(nv)], keep)
 
         @pl.when(has_high)
         def _():
@@ -342,24 +441,35 @@
                 leaving[i, at] = now[i] + q[i, planes - 1, padded(g)]
             forward_copy(g).start()
 
-    def sweep_down(g):
+    def sweep_down(g, now, known, keep=None):
         at = columns_of(g)
-        now = [following[v, at] for v in range(nv)]
         for x in reversed(range(planes)):
             now = [
-                prov[i, x, at] - total([eff[i, j, x, at] * now[j] for j in range(nv)])
+                known(i, x) - total([eff[i, j, x, at] * now[j] for j in range(nv)])
                 for i in range(nv)
             ]
-            if x == 0:
-                for i in range(nv):
-                    upd[i, at] = now[i]
-
-                @pl.when(has_low)
-                def _():
-                    backward_copy(g).start()
-
-            for i in range(nv):
-                state_out[0, i, x, at] = q[i, x, padded(g)] + now[i]
+            if keep is not None:
+                keep(x, now)
+        return now
+
+    nothing = jnp.zeros((GROUP, cells), jnp.float32)
+
+    def try_alone(g):
+        def keep(i, x, value):
+            trial[i, x] = value
+
+        climb(g, [nothing] * nv, keep)
+        now = sweep_down(g, [nothing] * nv, lambda i, x: trial[i, x])
+        for i in range(nv):
+            upd[i, columns_of(g)] = now[i]
+        backward_copy(g).start()
+
+    def applied(g, added, factor):
+        at = columns_of(g)
+        return [
+            total([added[i, at]] + [mats_in[i, j, at] * factor[j, at] for j in range(nv)])
+            for i in range(nv)
+        ]
 
     leads = both(rotor, slab <= 1)
     inside = groups - 2
@@ -392,19 +502,30 @@
                 pl.when(rotor_top)(functools.partial(gather_facing, above))
                 pl.when(stator_foot)(functools.partial(gather_facing, entering, below))
 
-            @pl.when(has_low)
+            pl.when(is_last)(functools.partial(try_alone, g))
+
+            @pl.when(both(has_low, has_high))
             def _():
                 forward_copy(g).wait_recv()
 
-            sweep_up(g)
-
-            @pl.when(is_last)
-            def _():
-                sweep_down(g)
+            pl.when(has_high)(functools.partial(sweep_up, g))
 
         return carry
 
     lax.fori_loop(0, groups + 2, advance, 0)
+
+    @pl.when(is_second)
+    def _():
+        def ahead(step, carry):
+            g = lax.rem(step + 1, groups)
+            at = columns_of(g)
+            now = sweep_down(g, [nothing] * nv, lambda i, x: prov[i, x, at])
+            for i in range(nv):
+                upd[i, at] = now[i]
+            base_copy(g).start()
+            return carry
+
+        lax.fori_loop(0, groups, ahead, 0)
 
     @pl.when(has_low)
     def _():
@@ -435,15 +556,55 @@
         for other in range(sectors):
             facing_copy(0, other).wait_send()
 
-    @pl.when(has_high)
-    def _():
-        def back(step, carry):
-            g = lax.rem(step + 1, groups)
+    def back(step, carry):
+        g = lax.rem(step + 1, groups)
+        at = columns_of(g)
+
+        @pl.when(is_last)
+        def _():
+            forward_copy(g).wait_recv()
+            sweep_up(g)
+
+        @pl.when(has_high)
+        def _():
             backward_copy(g).wait_recv()
-            sweep_down(g)
-            return carry
-
-        lax.fori_loop(0, groups, back, 0)
+
+        @pl.when(is_turn)
+        def _():
+            mat_copy(g).wait_recv()
+            now = applied(g, following, leaving)
+            for i in range(nv):
+                following[i, at] = now[i]
+
+        @pl.when(is_first)
+        def _():
+            mat_copy(g).wait_recv()
+            base_copy(g).wait_recv()
+            now = applied(g, base, following)
+            for i in range(nv):
+                following[i, at] = now[i]
+
+        def keep(x, now):
+            if x == 0:
+                @pl.when(both(slab >= 2, has_high))
+                def _():
+                    for i in range(nv):
+                        upd[i, at] = now[i]
+                    backward_copy(g).start()
+
+                    @pl.when(is_third)
+                    def _():
+                        skip_copy(g).start()
+
+            for i in range(nv):
+                state_out[0, i, x, at] = q[i, x, padded(g)] + now[i]
+
+        sweep_down(
+            g, [following[v, at] for v in range(nv)], lambda i, x: prov[i, x, at], keep
+        )
+        return carry
+
+    lax.fori_loop(0, groups, back, 0)
 
     def finish(g, carry):
         @pl.when(has_high)
@@ -453,6 +614,14 @@
         @pl.when(has_low)
         def _():
             backward_copy(g).wait_send()
+
+        @pl.when(is_third)
+        def _():
+            skip_copy(g).wait_send()
+
+        @pl.when(jnp.logical_or(is_last, is_second))
+        def _():
+            mat_copy(g).wait_send()
 
         return carry
 
@@ -506,9 +675,15 @@
             vmem(*plane),
             vmem(*plane),
             vmem(*plane),
+            vmem(*plane),
+            vmem(nv, *plane),
+            vmem(nv, *plane),
+            vmem(nv, nv, planes, GROUP, cells),
+            vmem(nv, planes, GROUP, cells),
             dma((7,)),
             dma((2,)), dma((2,)), dma((2,)), dma((2,)),
             dma((sectors,)), dma((sectors,)),
+            dma((groups,)), dma((groups,)), dma((groups,)), dma((groups,)),
             dma((groups,)), dma((groups,)), dma((groups,)), dma((groups,)),
             pltpu.SemaphoreType.REGULAR,
         ],

time: 33.1 us -> 29.3 us (0.89)
  Pallas kernels: 32.3 us -> 28.5 us
    pallas_call x1, Pallas kernels: 31.2 us -> 27.5 us  [per_device(): pl.pallas_call(functools.partial(kernel, sectors, slabs), out_shape=[vmem...]
where the time goes in v3:
time: 29.3 us; the launch traced here: 29.2 us
  Pallas kernels  28.5 us (97%)
  between operations  0.64 us (2%)
    pallas_call x1, Pallas kernels, per_device(): pl.pallas_call(functools.partial(kernel, sectors, slabs), out_shape=[vmem...  27.5 us
    pallas_call x1, Pallas kernels, per_device(): pl.pallas_call(write_out, out_shape=[jax.ShapeDtypeStruct(state.shape, jn...  1.07 us

profile of v3, /device:TPU:0, one launch (start us, length us, event | category | flops | bytes accessed | tf_op | source)
XLA Modules:
  0.0 29.2 jit_solution(8888707788101588402)
XLA Ops:
  0.6 27.5 %shard_map.77 = (f32[1,5,8,32,128]{4,3,2,1,0:T(8,128)S(1)}, f32[1,5,8,32,128]{4,3,2,1,0:T(8,128)S(1)}) custom-call(f32[1,5,8,32,128]{4,3,2,1,0:T(8,128)} %state.1, f32[1,5,8,32,128]{4,3,2,1,0:T(8,128)} %source.1, f32[1,5,5,8,32,128]{5,4,3,2,1,0:T(8,128)} %inverse.1, f32[5,1,5]{2,1,0:T(1,128)} %bitcast.4, f32[1,5,2,5]{3,2,1,0:T(2,128)} %bitcast.3, ...), custom_call_target="tpu_custom_call" | custom-call | tf_op jit(solution)/shard_map/pallas_call | solution.py:654
  28.1 1.1 %shard_map.78 = (f32[1,5,8,32,128]{4,3,2,1,0:T(8,128)}, f32[1,5,8,32,128]{4,3,2,1,0:T(8,128)}) custom-call(f32[1,5,8,32,128]{4,3,2,1,0:T(8,128)S(1)} %get-tuple-element.4.res_in, f32[1,5,8,32,128]{4,3,2,1,0:T(8,128)S(1)} %get-tuple-element.5.state_in), custom_call_target="tpu_custom_call" | custom-call | tf_op jit(solution)/shard_map/pallas_call | solution.py:693

commit v4 on v3

--- a/solution.py
+++ b/solution.py
@@ -34,7 +34,7 @@
     base, mats_out, mats_in, powers, trial,
     local_sem, ax_send, ax_recv, se_send, se_recv,
     if_send, if_recv, fw_send, fw_recv, bw_send, bw_recv,
-    skip_send, base_recv, mat_send, mat_recv, sectors_in,
+    skip_send, base_recv, mat_send, mat_recv, low_send, low_recv, sectors_in, turn_free,
 ):
     nv, planes, columns, cells = src.shape
     groups = columns // GROUP
@@ -57,7 +57,14 @@
     facing_slab = jnp.where(row == 0, 0, slabs - 1)
     body = pl.ds(PAD, columns)
 
-    load_state = pltpu.make_async_copy(state.at[0], q.at[:, :, body], local_sem.at[0])
+    def state_copy(first, count, at):
+        part = pl.ds(first, count)
+        return pltpu.make_async_copy(state.at[0, :, part], q.at[:, part, body], local_sem.at[at])
+
+    load_low, load_high = state_copy(0, 1, 0), state_copy(planes - 1, 1, 7)
+    load_state = state_copy(1, planes - 2, 8)
+    load_low.start()
+    load_high.start()
     load_state.start()
     load_axial = pltpu.make_async_copy(axial_in, axial, local_sem.at[4])
     load_axial.start()
@@ -77,14 +84,17 @@
 
     @pl.when(on_plane)
     def _():
-        for other in range(sectors):
-            greet(row=1 - row, sector=other, slab=facing_slab)
+        greet(row=1 - row, slab=facing_slab)
+        for step in range(1, sectors):
+            greet(sector=lax.rem(sector + step, sectors))
 
     @pl.when(has_high)
     def _():
         greet(slab=slab + 1)
 
-    @pl.when(jnp.logical_or(stator, outer))
+    beside = both(jnp.logical_or(stator, outer), jnp.logical_not(on_plane))
+
+    @pl.when(beside)
     def _():
         greet(sector=after)
         greet(sector=before)
@@ -95,45 +105,17 @@
         greet(row=1, sector=before)
         greet(row=1)
 
+    @pl.when(both(stator, is_last))
+    def _():
+        greet(row=0)
+
     peers = (
         has_low.astype(jnp.int32)
-        + jnp.where(jnp.logical_or(stator, outer), 2, 0)
+        + rotor_top.astype(jnp.int32)
+        + jnp.where(beside, 2, 0)
         + jnp.where(both(stator, middle), 3, 0)
         + jnp.where(on_plane, sectors, 0)
     )
-
-    zero_plane = jnp.zeros((nv, columns, cells), jnp.float32)
-    zero_columns = jnp.zeros((nv, planes, PAD, cells), jnp.float32)
-    q[:, :, pl.ds(0, PAD)] = zero_columns
-    q[:, :, pl.ds(PAD + columns, PAD)] = zero_columns
-
-    @pl.when(is_first)
-    def _():
-        entering[...] = zero_plane
-        below[...] = zero_plane
-
-    @pl.when(is_last)
-    def _():
-        following[...] = zero_plane
-        above[...] = zero_plane
-
-    move_picks = pltpu.make_async_copy(picks_wide, picks, local_sem.at[6])
-    load_owner.wait()
-
-    @pl.when(on_plane)
-    def _():
-        shape = (columns, owner.shape[1])
-        ids = sector * columns + lax.broadcasted_iota(jnp.int32, shape, 0)
-        everyone = lax.broadcasted_iota(jnp.int32, shape, 1)
-        owners = jnp.broadcast_to(owner[...], shape)
-        is_rotor = jnp.broadcast_to(row, shape) == 0
-        hits = jnp.where(is_rotor, everyone, owners) == ids
-        found = jnp.sum(
-            jnp.where(hits, jnp.where(is_rotor, owners, everyone), 0), axis=1, keepdims=True
-        )
-        found = jnp.minimum(found, owner.shape[1] - 1)
-        picks_wide[...] = jnp.broadcast_to(found, picks_wide.shape)
-        move_picks.start()
 
     def remote(source_ref, target_ref, send, recv, **where):
         return pltpu.make_async_remote_copy(
@@ -141,16 +123,29 @@
             device_id=where, device_id_type=MESH,
         )
 
-    def facing_copy(plane_at, other):
-        return remote(
-            q.at[:, plane_at, body], facing.at[sector], if_send.at[other], if_recv.at[sector],
-            row=1 - row, sector=other, slab=facing_slab,
-        )
-
-    def facing_arrival(other):
-        return remote(
-            q.at[:, 0, body], facing.at[other], if_send.at[other], if_recv.at[other],
-            row=1 - row, sector=other, slab=facing_slab,
+    def columns_of(g):
+        return pl.ds(pl.multiple_of(g * GROUP, GROUP), GROUP)
+
+    def padded(g):
+        return pl.ds(pl.multiple_of(PAD + g * GROUP, GROUP), GROUP)
+
+    def facing_copy(plane_at):
+        return remote(
+            q.at[:, plane_at, body], facing.at[sector], if_send.at[0], if_recv.at[sector],
+            row=1 - row, slab=facing_slab,
+        )
+
+    def facing_relay(step):
+        return remote(
+            facing.at[sector], facing.at[sector], if_send.at[step], if_recv.at[sector],
+            sector=lax.rem(sector + step, sectors),
+        )
+
+    def facing_arrival(step):
+        origin = lax.rem(sector + step, sectors)
+        return remote(
+            facing.at[origin], facing.at[origin], if_send.at[step], if_recv.at[origin],
+            sector=origin,
         )
 
     to_after = remote(
@@ -170,9 +165,28 @@
     to_high = remote(
         q.at[:, planes - 1, body], below, ax_send.at[0], ax_recv.at[0], slab=slab + 1
     )
-    to_low = remote(
-        q.at[:, 0, body], above, ax_send.at[1], ax_recv.at[1], slab=slab - 1
-    )
+
+    def low_copy(g):
+        return remote(
+            q.at[:, 0, padded(g)], above.at[:, columns_of(g)],
+            low_send.at[g], low_recv.at[g], slab=slab - 1,
+        )
+
+    def clear():
+        zero_plane = jnp.zeros((nv, columns, cells), jnp.float32)
+        zero_columns = jnp.zeros((nv, planes, PAD, cells), jnp.float32)
+        q[:, :, pl.ds(0, PAD)] = zero_columns
+        q[:, :, pl.ds(PAD + columns, PAD)] = zero_columns
+
+        @pl.when(is_first)
+        def _():
+            entering[...] = zero_plane
+            below[...] = zero_plane
+
+        @pl.when(is_last)
+        def _():
+            following[...] = zero_plane
+            above[...] = zero_plane
 
     at_start = sector == 0
 
@@ -181,17 +195,16 @@
 
         @pl.when(has_low)
         def _():
-            to_low.start()
+            for step in range(groups):
+                low_copy((step + 1) % groups).start()
 
         @pl.when(rotor_top)
         def _():
-            for other in range(sectors):
-                facing_copy(planes - 1, other).start()
+            facing_copy(planes - 1).start()
 
         @pl.when(stator_foot)
         def _():
-            for other in range(sectors):
-                facing_copy(0, other).start()
+            facing_copy(0).start()
 
         @pl.when(both(stator, middle))
         def _():
@@ -206,12 +219,6 @@
 
         to_after.start()
         to_before.start()
-
-    def columns_of(g):
-        return pl.ds(pl.multiple_of(g * GROUP, GROUP), GROUP)
-
-    def padded(g):
-        return pl.ds(pl.multiple_of(PAD + g * GROUP, GROUP), GROUP)
 
     lane = lax.broadcasted_iota(jnp.int32, (columns, cells), 1)
     no_cells = jnp.zeros((columns, cells), jnp.float32)
@@ -256,17 +263,42 @@
         lax.fori_loop(0, planes, flux, 0)
 
     early = jnp.logical_or(jnp.logical_not(at_start), both(rotor, middle))
-    opens_at = jnp.where(early, 0, 2)
-    meets_at = jnp.where(at_start, 2, 0)
-    load_state.wait()
+    opens_at = jnp.where(early, 0, 3)
+    meets_at = jnp.where(at_start, 3, 1)
+    load_low.wait()
+    load_high.wait()
 
     def prepare(step, carry):
         pl.when(step == opens_at)(open_up)
+
+        @pl.when(step == 1)
+        def _():
+            clear()
+            load_state.wait()
+
         pl.when(step == meets_at)(meet_sectors)
-        pl.when(step == 1)(local_work)
+        pl.when(step == 2)(local_work)
         return carry
 
-    lax.fori_loop(0, 3, prepare, 0)
+    lax.fori_loop(0, 4, prepare, 0)
+    move_picks = pltpu.make_async_copy(picks_wide, picks, local_sem.at[6])
+    load_owner.wait()
+
+    @pl.when(on_plane)
+    def _():
+        shape = (columns, owner.shape[1])
+        ids = sector * columns + lax.broadcasted_iota(jnp.int32, shape, 0)
+        everyone = lax.broadcasted_iota(jnp.int32, shape, 1)
+        owners = jnp.broadcast_to(owner[...], shape)
+        is_rotor = jnp.broadcast_to(row, shape) == 0
+        hits = jnp.where(is_rotor, everyone, owners) == ids
+        found = jnp.sum(
+            jnp.where(hits, jnp.where(is_rotor, owners, everyone), 0), axis=1, keepdims=True
+        )
+        found = jnp.minimum(found, owner.shape[1] - 1)
+        picks_wide[...] = jnp.broadcast_to(found, picks_wide.shape)
+        move_picks.start()
+
     place = lax.broadcasted_iota(jnp.int32, (GROUP, cells), 0)
 
     def mend(side):
@@ -299,8 +331,8 @@
 
     def gather_facing(*targets):
         move_picks.wait()
-        for other in range(sectors):
-            facing_arrival(other).wait_recv()
+        for step in range(1, sectors):
+            facing_arrival(step).wait_recv()
 
         def pick(block, carry):
             for inner in range(GROUP):
@@ -360,13 +392,16 @@
     def unpack(values):
         return [list(values[i * nv : i * nv + nv]) for i in range(nv)]
 
-    def send_matrix(g, values):
+    def store_matrix(g, values):
         at = columns_of(g)
         matrix = unpack(values)
         for i in range(nv):
             for k in range(nv):
                 mats_out[i, k, at] = matrix[i][k]
-        mat_copy(g).start()
+
+        @pl.when(jnp.logical_or(rotor_top, both(stator, is_second)))
+        def _():
+            mat_copy(g).start()
 
     def entry_to_update(step, carry):
         g = lax.rem(step + 1, groups)
@@ -391,7 +426,7 @@
             )
 
         values = lax.fori_loop(1, planes, up, pack(first))
-        send_matrix(g, lax.fori_loop(0, planes - 1, down, values))
+        store_matrix(g, lax.fori_loop(0, planes - 1, down, values))
         return carry
 
     def exit_to_update(step, carry):
@@ -403,7 +438,7 @@
             return pack([[-value for value in line] for line in product])
 
         last = [[-value for value in line] for line in blocks_at(planes - 1, at)]
-        send_matrix(g, lax.fori_loop(0, planes - 1, down, pack(last)))
+        store_matrix(g, lax.fori_loop(0, planes - 1, down, pack(last)))
         return carry
 
     @pl.when(is_last)
@@ -471,6 +506,26 @@
             for i in range(nv)
         ]
 
+    @pl.when(on_plane)
+    def _():
+        facing_copy(0).wait_recv()
+        for step in range(1, sectors):
+            facing_relay(step).start()
+
+    @pl.when(is_last)
+    def _():
+        @pl.when(rotor)
+        def _():
+            for g in range(groups):
+                mat_copy(g).wait_send()
+            pl.semaphore_signal(turn_free, inc=1, device_id=dict(row=1), device_id_type=MESH)
+
+        @pl.when(stator)
+        def _():
+            pl.semaphore_wait(turn_free, 1)
+            for step in range(groups):
+                mat_copy((step + 1) % groups).start()
+
     leads = both(rotor, slab <= 1)
     inside = groups - 2
 
@@ -494,15 +549,18 @@
 
             @pl.when(sweep_at == 0)
             def _():
-                @pl.when(has_high)
-                def _():
-                    to_low.wait_recv()
-                    to_high.start()
-
                 pl.when(rotor_top)(functools.partial(gather_facing, above))
                 pl.when(stator_foot)(functools.partial(gather_facing, entering, below))
 
             pl.when(is_last)(functools.partial(try_alone, g))
+
+            @pl.when(has_high)
+            def _():
+                low_copy(g).wait_recv()
+
+            @pl.when(both(has_high, sweep_at == 0))
+            def _():
+                to_high.start()
 
             @pl.when(both(has_low, has_high))
             def _():
@@ -523,6 +581,11 @@
             for i in range(nv):
                 upd[i, at] = now[i]
             base_copy(g).start()
+
+            @pl.when(rotor)
+            def _():
+                mat_copy(g).start()
+
             return carry
 
         lax.fori_loop(0, groups, ahead, 0)
@@ -549,12 +612,14 @@
 
     @pl.when(has_low)
     def _():
-        to_low.wait_send()
+        for g in range(groups):
+            low_copy(g).wait_send()
 
     @pl.when(on_plane)
     def _():
-        for other in range(sectors):
-            facing_copy(0, other).wait_send()
+        facing_copy(0).wait_send()
+        for step in range(1, sectors):
+            facing_relay(step).wait_send()
 
     def back(step, carry):
         g = lax.rem(step + 1, groups)
@@ -619,7 +684,7 @@
         def _():
             skip_copy(g).wait_send()
 
-        @pl.when(jnp.logical_or(is_last, is_second))
+        @pl.when(jnp.logical_or(both(stator, is_last), is_second))
         def _():
             mat_copy(g).wait_send()
 
@@ -680,11 +745,13 @@
             vmem(nv, *plane),
             vmem(nv, nv, planes, GROUP, cells),
             vmem(nv, planes, GROUP, cells),
-            dma((7,)),
-            dma((2,)), dma((2,)), dma((2,)), dma((2,)),
+            dma((9,)),
+            dma((1,)), dma((1,)), dma((2,)), dma((2,)),
             dma((sectors,)), dma((sectors,)),
             dma((groups,)), dma((groups,)), dma((groups,)), dma((groups,)),
             dma((groups,)), dma((groups,)), dma((groups,)), dma((groups,)),
+            dma((groups,)), dma((groups,)),
+            pltpu.SemaphoreType.REGULAR,
             pltpu.SemaphoreType.REGULAR,
         ],
         compiler_params=pltpu.CompilerParams(collective_id=0, has_side_effects=True),

time: 29.3 us -> 26.9 us (0.918)
  the two profiles are of different devices: /device:TPU:0 before, /device:TPU:1 now
where the time goes in v4:
time: 26.9 us; the launch traced here: 26.8 us
  Pallas kernels  26.1 us (97%)
  between operations  0.64 us (2%)
    pallas_call x1, Pallas kernels, per_device(): pl.pallas_call(functools.partial(kernel, sectors, slabs), out_shape=[vmem...  25 us
    pallas_call x1, Pallas kernels, per_device(): pl.pallas_call(write_out, out_shape=[jax.ShapeDtypeStruct(state.shape, jn...  1.07 us

profile of v4, /device:TPU:1, one launch (start us, length us, event | category | flops | bytes accessed | tf_op | source)
XLA Modules:
  0.0 26.8 jit_solution(11031846172157198873)
XLA Ops:
  0.6 25.0 %shard_map.77 = (f32[1,5,8,32,128]{4,3,2,1,0:T(8,128)S(1)}, f32[1,5,8,32,128]{4,3,2,1,0:T(8,128)S(1)}) custom-call(f32[1,5,8,32,128]{4,3,2,1,0:T(8,128)} %state.1, f32[1,5,8,32,128]{4,3,2,1,0:T(8,128)} %source.1, f32[1,5,5,8,32,128]{5,4,3,2,1,0:T(8,128)} %inverse.1, f32[5,1,5]{2,1,0:T(1,128)} %bitcast.4, f32[1,5,2,5]{3,2,1,0:T(2,128)} %bitcast.3, ...), custom_call_target="tpu_custom_call" | custom-call | tf_op jit(solution)/shard_map/pallas_call | solution.py:719
  25.7 1.1 %shard_map.78 = (f32[1,5,8,32,128]{4,3,2,1,0:T(8,128)}, f32[1,5,8,32,128]{4,3,2,1,0:T(8,128)}) custom-call(f32[1,5,8,32,128]{4,3,2,1,0:T(8,128)S(1)} %get-tuple-element.4.res_in, f32[1,5,8,32,128]{4,3,2,1,0:T(8,128)S(1)} %get-tuple-element.5.state_in), custom_call_target="tpu_custom_call" | custom-call | tf_op jit(solution)/shard_map/pallas_call | solution.py:760

commit v5 on v2

--- a/solution.py
+++ b/solution.py
@@ -31,8 +31,10 @@
     res_out, state_out,
     axial, cross, owner, picks_wide, picks,
     q, halo, src, inv, eff, prov, below, above, facing, entering, following, leaving, upd,
+    base, mats_out, mats_in, powers, trial,
     local_sem, ax_send, ax_recv, se_send, se_recv,
-    if_send, if_recv, fw_send, fw_recv, bw_send, bw_recv, sectors_in,
+    if_send, if_recv, fw_send, fw_recv, bw_send, bw_recv,
+    skip_send, base_recv, mat_send, mat_recv, low_send, low_recv, inverse_sem, sectors_in,
 ):
     nv, planes, columns, cells = src.shape
     groups = columns // GROUP
@@ -43,6 +45,8 @@
     has_low = slab > 0
     has_high = slab < slabs - 1
     is_first, is_last = slab == 0, slab == slabs - 1
+    is_second, is_third = slab == 1, slab == 2
+    is_turn = slab == slabs - 2
     middle = both(has_low, has_high)
     outer = jnp.logical_or(is_first, is_last)
     rotor_top = both(rotor, is_last)
@@ -53,12 +57,23 @@
     facing_slab = jnp.where(row == 0, 0, slabs - 1)
     body = pl.ds(PAD, columns)
 
-    load_state = pltpu.make_async_copy(state.at[0], q.at[:, :, body], local_sem.at[0])
-    load_state.start()
+    def state_copy(first, count, at):
+        part = pl.ds(first, count)
+        return pltpu.make_async_copy(state.at[0, :, part], q.at[:, part, body], local_sem.at[at])
+
+    load_low, load_high = state_copy(0, 1, 0), state_copy(planes - 1, 1, 7)
+    load_state = state_copy(1, planes - 2, 8)
+    load_low.start()
+    load_high.start()
     load_axial = pltpu.make_async_copy(axial_in, axial, local_sem.at[4])
     load_axial.start()
-    load_inverse = pltpu.make_async_copy(inverse.at[0], inv, local_sem.at[2])
-    load_inverse.start()
+
+    def inverse_copy(x):
+        return pltpu.make_async_copy(inverse.at[0, :, :, x], inv.at[:, :, x], inverse_sem.at[x])
+
+    for x in range(planes):
+        inverse_copy(x).start()
+    load_state.start()
     load_cross = pltpu.make_async_copy(cross_in, cross, local_sem.at[5])
     load_cross.start()
     load_owner = pltpu.make_async_copy(owner_in, owner, local_sem.at[3])
@@ -73,14 +88,17 @@
 
     @pl.when(on_plane)
     def _():
-        for other in range(sectors):
-            greet(row=1 - row, sector=other, slab=facing_slab)
+        greet(row=1 - row, slab=facing_slab)
+        for step in range(1, sectors):
+            greet(sector=lax.rem(sector + step, sectors))
 
     @pl.when(has_high)
     def _():
         greet(slab=slab + 1)
 
-    @pl.when(jnp.logical_or(stator, outer))
+    beside = both(jnp.logical_or(stator, outer), jnp.logical_not(on_plane))
+
+    @pl.when(beside)
     def _():
         greet(sector=after)
         greet(sector=before)
@@ -93,43 +111,10 @@
 
     peers = (
         has_low.astype(jnp.int32)
-        + jnp.where(jnp.logical_or(stator, outer), 2, 0)
+        + jnp.where(beside, 2, 0)
         + jnp.where(both(stator, middle), 3, 0)
         + jnp.where(on_plane, sectors, 0)
     )
-
-    zero_plane = jnp.zeros((nv, columns, cells), jnp.float32)
-    zero_columns = jnp.zeros((nv, planes, PAD, cells), jnp.float32)
-    q[:, :, pl.ds(0, PAD)] = zero_columns
-    q[:, :, pl.ds(PAD + columns, PAD)] = zero_columns
-
-    @pl.when(is_first)
-    def _():
-        entering[...] = zero_plane
-        below[...] = zero_plane
-
-    @pl.when(is_last)
-    def _():
-        following[...] = zero_plane
-        above[...] = zero_plane
-
-    move_picks = pltpu.make_async_copy(picks_wide, picks, local_sem.at[6])
-    load_owner.wait()
-
-    @pl.when(on_plane)
-    def _():
-        shape = (columns, owner.shape[1])
-        ids = sector * columns + lax.broadcasted_iota(jnp.int32, shape, 0)
-        everyone = lax.broadcasted_iota(jnp.int32, shape, 1)
-        owners = jnp.broadcast_to(owner[...], shape)
-        is_rotor = jnp.broadcast_to(row, shape) == 0
-        hits = jnp.where(is_rotor, everyone, owners) == ids
-        found = jnp.sum(
-            jnp.where(hits, jnp.where(is_rotor, owners, everyone), 0), axis=1, keepdims=True
-        )
-        found = jnp.minimum(found, owner.shape[1] - 1)
-        picks_wide[...] = jnp.broadcast_to(found, picks_wide.shape)
-        move_picks.start()
 
     def remote(source_ref, target_ref, send, recv, **where):
         return pltpu.make_async_remote_copy(
@@ -137,17 +122,37 @@
             device_id=where, device_id_type=MESH,
         )
 
-    def facing_copy(plane_at, other):
+    def columns_of(g):
+        return pl.ds(pl.multiple_of(g * GROUP, GROUP), GROUP)
+
+    def padded(g):
+        return pl.ds(pl.multiple_of(PAD + g * GROUP, GROUP), GROUP)
+
+    def facing_copy(plane_at, g):
         return remote(
-            q.at[:, plane_at, body], facing.at[sector], if_send.at[other], if_recv.at[sector],
-            row=1 - row, sector=other, slab=facing_slab,
-        )
-
-    def facing_arrival(other):
+            q.at[:, plane_at, padded(g)], facing.at[sector, :, columns_of(g)],
+            if_send.at[0, g], if_recv.at[sector, g], row=1 - row, slab=facing_slab,
+        )
+
+    def facing_relay(step, g):
+        part = facing.at[sector, :, columns_of(g)]
         return remote(
-            q.at[:, 0, body], facing.at[other], if_send.at[other], if_recv.at[other],
-            row=1 - row, sector=other, slab=facing_slab,
-        )
+            part, part, if_send.at[step, g], if_recv.at[sector, g],
+            sector=lax.rem(sector + step, sectors),
+        )
+
+    def facing_arrival(step, g):
+        origin = lax.rem(sector + step, sectors)
+        part = facing.at[origin, :, columns_of(g)]
+        return remote(part, part, if_send.at[step, g], if_recv.at[origin, g], sector=origin)
+
+    def per_piece(action):
+        def one(step, carry):
+            for g in range(groups):
+                action(step, g)
+            return carry
+
+        lax.fori_loop(1, sectors, one, 0)
 
     to_after = remote(
         q.at[:, :, pl.ds(PAD + columns - 1, 1)], halo.at[0],
@@ -166,9 +171,28 @@
     to_high = remote(
         q.at[:, planes - 1, body], below, ax_send.at[0], ax_recv.at[0], slab=slab + 1
     )
-    to_low = remote(
-        q.at[:, 0, body], above, ax_send.at[1], ax_recv.at[1], slab=slab - 1
-    )
+
+    def low_copy(g):
+        return remote(
+            q.at[:, 0, padded(g)], above.at[:, columns_of(g)],
+            low_send.at[g], low_recv.at[g], slab=slab - 1,
+        )
+
+    def clear():
+        zero_plane = jnp.zeros((nv, columns, cells), jnp.float32)
+        zero_columns = jnp.zeros((nv, planes, PAD, cells), jnp.float32)
+        q[:, :, pl.ds(0, PAD)] = zero_columns
+        q[:, :, pl.ds(PAD + columns, PAD)] = zero_columns
+
+        @pl.when(is_first)
+        def _():
+            entering[...] = zero_plane
+            below[...] = zero_plane
+
+        @pl.when(is_last)
+        def _():
+            following[...] = zero_plane
+            above[...] = zero_plane
 
     at_start = sector == 0
 
@@ -177,17 +201,18 @@
 
         @pl.when(has_low)
         def _():
-            to_low.start()
+            for step in range(groups):
+                low_copy((step + 1) % groups).start()
 
         @pl.when(rotor_top)
         def _():
-            for other in range(sectors):
-                facing_copy(planes - 1, other).start()
+            for g in range(groups):
+                facing_copy(planes - 1, g).start()
 
         @pl.when(stator_foot)
         def _():
-            for other in range(sectors):
-                facing_copy(0, other).start()
+            for g in range(groups):
+                facing_copy(0, g).start()
 
         @pl.when(both(stator, middle))
         def _():
@@ -203,16 +228,11 @@
         to_after.start()
         to_before.start()
 
-    def columns_of(g):
-        return pl.ds(pl.multiple_of(g * GROUP, GROUP), GROUP)
-
-    def padded(g):
-        return pl.ds(pl.multiple_of(PAD + g * GROUP, GROUP), GROUP)
-
     lane = lax.broadcasted_iota(jnp.int32, (columns, cells), 1)
     no_cells = jnp.zeros((columns, cells), jnp.float32)
 
     def effective(x, carry):
+        inverse_copy(x).wait()
         for i in range(nv):
             blocks = [inv[i, j, x] for j in range(nv)]
             for k in range(nv):
@@ -243,26 +263,147 @@
             prov[i, x] = total([inv[i, j, x] * values[j] for j in range(nv)])
         return carry
 
-    def local_work():
+    def mat_copy(g):
+        return remote(
+            mats_out.at[:, :, columns_of(g)], mats_in.at[:, :, columns_of(g)],
+            mat_send.at[g], mat_recv.at[g], slab=slab - 1,
+        )
+
+    def blocks_at(x, at):
+        return [[eff[i, j, x, at] for j in range(nv)] for i in range(nv)]
+
+    def times(left, right):
+        return [
+            [total([left[i][j] * right[j][k] for j in range(nv)]) for k in range(nv)]
+            for i in range(nv)
+        ]
+
+    def pack(matrix):
+        return tuple(matrix[i][k] for i in range(nv) for k in range(nv))
+
+    def unpack(values):
+        return [list(values[i * nv : i * nv + nv]) for i in range(nv)]
+
+    def store_matrix(g, values):
+        at = columns_of(g)
+        matrix = unpack(values)
+        for i in range(nv):
+            for k in range(nv):
+                mats_out[i, k, at] = matrix[i][k]
+
+        @pl.when(jnp.logical_or(rotor_top, both(stator, is_second)))
+        def _():
+            mat_copy(g).start()
+
+    def entry_to_update(step, carry):
+        g = lax.rem(step + 1, groups)
+        at = columns_of(g)
+        first = blocks_at(0, at)
+        for i in range(nv):
+            for k in range(nv):
+                powers[i, k, 0] = first[i][k]
+
+        def up(x, values):
+            product = times(blocks_at(x, at), unpack(values))
+            for i in range(nv):
+                for k in range(nv):
+                    powers[i, k, x] = product[i][k]
+            return pack(product)
+
+        def down(step, values):
+            x = planes - 2 - step
+            product = times(blocks_at(x, at), unpack(values))
+            return pack(
+                [[powers[i, k, x] - product[i][k] for k in range(nv)] for i in range(nv)]
+            )
+
+        values = lax.fori_loop(1, planes, up, pack(first))
+        store_matrix(g, lax.fori_loop(0, planes - 1, down, values))
+        return carry
+
+    def exit_to_update(step, carry):
+        g = lax.rem(step + 1, groups)
+        at = columns_of(g)
+
+        def down(step, values):
+            product = times(blocks_at(planes - 2 - step, at), unpack(values))
+            return pack([[-value for value in line] for line in product])
+
+        last = [[-value for value in line] for line in blocks_at(planes - 1, at)]
+        store_matrix(g, lax.fori_loop(0, planes - 1, down, pack(last)))
+        return carry
+
+    def pass_on():
+        def one(g, carry):
+            facing_copy(0, g).wait_recv()
+
+            def start(step, carry):
+                facing_relay(step, g).start()
+                return carry
+
+            return lax.fori_loop(1, sectors, start, carry)
+
+        lax.fori_loop(0, groups, one, 0)
+
+    def matrices():
+        @pl.when(is_last)
+        def _():
+            lax.fori_loop(0, groups, entry_to_update, 0)
+
+        @pl.when(is_second)
+        def _():
+            lax.fori_loop(0, groups, exit_to_update, 0)
+
+    def products():
         load_axial.wait()
-        load_inverse.wait()
         lax.fori_loop(0, planes, effective, 0)
+
+    def fluxes():
         load_cross.wait()
         load_source.wait()
         lax.fori_loop(0, planes, flux, 0)
 
     early = jnp.logical_or(jnp.logical_not(at_start), both(rotor, middle))
-    opens_at = jnp.where(early, 0, 2)
-    meets_at = jnp.where(at_start, 2, 0)
-    load_state.wait()
+    opens_at = jnp.where(early, 0, jnp.where(has_low, 3, 6))
+    meets_at = jnp.where(at_start, 6, 1)
+    passes_at = jnp.where(opens_at > 5, 7, 5)
+    load_low.wait()
+    load_high.wait()
 
     def prepare(step, carry):
         pl.when(step == opens_at)(open_up)
+
+        @pl.when(step == 1)
+        def _():
+            clear()
+            load_state.wait()
+
         pl.when(step == meets_at)(meet_sectors)
-        pl.when(step == 1)(local_work)
+        pl.when(step == 2)(products)
+        pl.when(step == 4)(matrices)
+        pl.when(both(step == passes_at, on_plane))(pass_on)
+        pl.when(step == 5)(fluxes)
         return carry
 
-    lax.fori_loop(0, 3, prepare, 0)
+    lax.fori_loop(0, 8, prepare, 0)
+    move_picks = pltpu.make_async_copy(picks_wide, picks, local_sem.at[6])
+    load_owner.wait()
+
+    @pl.when(on_plane)
+    def _():
+        shape = (columns, owner.shape[1])
+        ids = sector * columns + lax.broadcasted_iota(jnp.int32, shape, 0)
+        everyone = lax.broadcasted_iota(jnp.int32, shape, 1)
+        owners = jnp.broadcast_to(owner[...], shape)
+        is_rotor = jnp.broadcast_to(row, shape) == 0
+        hits = jnp.where(is_rotor, everyone, owners) == ids
+        found = jnp.sum(
+            jnp.where(hits, jnp.where(is_rotor, owners, everyone), 0), axis=1, keepdims=True
+        )
+        found = jnp.minimum(found, owner.shape[1] - 1)
+        picks_wide[...] = jnp.broadcast_to(found, picks_wide.shape)
+        move_picks.start()
+
     place = lax.broadcasted_iota(jnp.int32, (GROUP, cells), 0)
 
     def mend(side):
@@ -295,8 +436,7 @@
 
     def gather_facing(*targets):
         move_picks.wait()
-        for other in range(sectors):
-            facing_arrival(other).wait_recv()
+        per_piece(lambda step, g: facing_arrival(step, g).wait_recv())
 
         def pick(block, carry):
             for inner in range(GROUP):
@@ -323,9 +463,20 @@
             bw_send.at[g], bw_recv.at[g], slab=slab - 1,
         )
 
-    def sweep_up(g):
-        at = columns_of(g)
-        now = [entering[v, at] for v in range(nv)]
+    def skip_copy(g):
+        return remote(
+            upd.at[:, columns_of(g)], following.at[:, columns_of(g)],
+            skip_send.at[g], bw_recv.at[g], slab=0,
+        )
+
+    def base_copy(g):
+        return remote(
+            upd.at[:, columns_of(g)], base.at[:, columns_of(g)],
+            bw_send.at[g], base_recv.at[g], slab=0,
+        )
+
+    def climb(g, now, keep):
+        at = columns_of(g)
         for x in range(planes):
             if x == planes - 1:
                 now = [now[v] - above[v, at] for v in range(nv)]
@@ -334,7 +485,16 @@
                 for i in range(nv)
             ]
             for i in range(nv):
-                prov[i, x, at] = now[i]
+                keep(i, x, now[i])
+        return now
+
+    def sweep_up(g):
+        at = columns_of(g)
+
+        def keep(i, x, value):
+            prov[i, x, at] = value
+
+        now = climb(g, [entering[v, at] for v in range(nv)], keep)
 
         @pl.when(has_high)
         def _():
@@ -342,24 +502,91 @@
                 leaving[i, at] = now[i] + q[i, planes - 1, padded(g)]
             forward_copy(g).start()
 
-    def sweep_down(g):
-        at = columns_of(g)
-        now = [following[v, at] for v in range(nv)]
+    def sweep_down(g, now, known, keep=None):
+        at = columns_of(g)
         for x in reversed(range(planes)):
             now = [
-                prov[i, x, at] - total([eff[i, j, x, at] * now[j] for j in range(nv)])
+                known(i, x) - total([eff[i, j, x, at] * now[j] for j in range(nv)])
                 for i in range(nv)
             ]
+            if keep is not None:
+                keep(x, now)
+        return now
+
+    nothing = jnp.zeros((GROUP, cells), jnp.float32)
+
+    def climb_alone(g):
+        at = columns_of(g)
+
+        def keep(i, x, value):
+            trial[i, x, at] = value
+
+        climb(g, [nothing] * nv, keep)
+
+    def descend_alone(step, carry):
+        g = lax.rem(step + 1, groups)
+        at = columns_of(g)
+        now = sweep_down(
+            g, [following[v, at] for v in range(nv)], lambda i, x: trial[i, x, at]
+        )
+        for i in range(nv):
+            upd[i, at] = now[i]
+        backward_copy(g).start()
+        return carry
+
+    def applied(g, added, factor):
+        at = columns_of(g)
+        return [
+            total([added[i, at]] + [mats_in[i, j, at] * factor[j, at] for j in range(nv)])
+            for i in range(nv)
+        ]
+
+    at_once = both(stator, is_turn)
+    def finish_group(g):
+        at = columns_of(g)
+
+        @pl.when(is_last)
+        def _():
+            forward_copy(g).wait_recv()
+            sweep_up(g)
+
+        @pl.when(has_high)
+        def _():
+            backward_copy(g).wait_recv()
+
+        @pl.when(is_turn)
+        def _():
+            mat_copy(g).wait_recv()
+            now = applied(g, following, leaving)
+            for i in range(nv):
+                following[i, at] = now[i]
+
+        @pl.when(is_first)
+        def _():
+            mat_copy(g).wait_recv()
+            base_copy(g).wait_recv()
+            now = applied(g, base, following)
+            for i in range(nv):
+                following[i, at] = now[i]
+
+        def keep(x, now):
             if x == 0:
-                for i in range(nv):
-                    upd[i, at] = now[i]
-
-                @pl.when(has_low)
+                @pl.when(both(slab >= 2, has_high))
                 def _():
+                    for i in range(nv):
+                        upd[i, at] = now[i]
                     backward_copy(g).start()
 
+                    @pl.when(is_third)
+                    def _():
+                        skip_copy(g).start()
+
             for i in range(nv):
                 state_out[0, i, x, at] = q[i, x, padded(g)] + now[i]
+
+        sweep_down(
+            g, [following[v, at] for v in range(nv)], lambda i, x: prov[i, x, at], keep
+        )
 
     leads = both(rotor, slab <= 1)
     inside = groups - 2
@@ -384,27 +611,56 @@
 
             @pl.when(sweep_at == 0)
             def _():
-                @pl.when(has_high)
-                def _():
-                    to_low.wait_recv()
-                    to_high.start()
-
-                pl.when(rotor_top)(functools.partial(gather_facing, above))
                 pl.when(stator_foot)(functools.partial(gather_facing, entering, below))
 
-            @pl.when(has_low)
+            pl.when(is_last)(functools.partial(climb_alone, g))
+
+            @pl.when(has_high)
+            def _():
+                low_copy(g).wait_recv()
+
+            @pl.when(both(has_high, sweep_at == 0))
+            def _():
+                to_high.start()
+
+            @pl.when(both(has_low, has_high))
             def _():
                 forward_copy(g).wait_recv()
 
-            sweep_up(g)
-
-            @pl.when(is_last)
+            pl.when(has_high)(functools.partial(sweep_up, g))
+            pl.when(at_once)(functools.partial(finish_group, g))
+
+        return carry
+
+    lax.fori_loop(0, groups + 2, advance, 0)
+
+    @pl.when(is_last)
+    def _():
+        pl.when(rotor)(functools.partial(gather_facing, following))
+        lax.fori_loop(0, groups, descend_alone, 0)
+
+        @pl.when(stator)
+        def _():
+            for step in range(groups):
+                mat_copy((step + 1) % groups).start()
+
+    @pl.when(is_second)
+    def _():
+        def ahead(step, carry):
+            g = lax.rem(step + 1, groups)
+            at = columns_of(g)
+            now = sweep_down(g, [nothing] * nv, lambda i, x: prov[i, x, at])
+            for i in range(nv):
+                upd[i, at] = now[i]
+            base_copy(g).start()
+
+            @pl.when(rotor)
             def _():
-                sweep_down(g)
-
-        return carry
-
-    lax.fori_loop(0, groups + 2, advance, 0)
+                mat_copy(g).start()
+
+            return carry
+
+        lax.fori_loop(0, groups, ahead, 0)
 
     @pl.when(has_low)
     def _():
@@ -414,10 +670,14 @@
         res_out[0, i, 0] = res_out[0, i, 0] + total(
             [(0.5 * axial[i, 0, j]) * below[j] for j in range(nv)]
         )
-    for i in range(nv):
-        res_out[0, i, planes - 1] = res_out[0, i, planes - 1] - total(
-            [(0.5 * axial[i, 0, j]) * above[j] for j in range(nv)]
-        )
+    def mend_top(beyond):
+        for i in range(nv):
+            res_out[0, i, planes - 1] = res_out[0, i, planes - 1] - total(
+                [(0.5 * axial[i, 0, j]) * beyond[j] for j in range(nv)]
+            )
+
+    pl.when(is_last)(functools.partial(mend_top, following))
+    pl.when(has_high)(functools.partial(mend_top, above))
 
     to_after.wait_send()
     to_before.wait_send()
@@ -428,22 +688,23 @@
 
     @pl.when(has_low)
     def _():
-        to_low.wait_send()
+        for g in range(groups):
+            low_copy(g).wait_send()
 
     @pl.when(on_plane)
     def _():
-        for other in range(sectors):
-            facing_copy(0, other).wait_send()
-
-    @pl.when(has_high)
-    def _():
-        def back(step, carry):
-            g = lax.rem(step + 1, groups)
-            backward_copy(g).wait_recv()
-            sweep_down(g)
-            return carry
-
-        lax.fori_loop(0, groups, back, 0)
+        for g in range(groups):
+            facing_copy(0, g).wait_send()
+        per_piece(lambda step, g: facing_relay(step, g).wait_send())
+
+    def back(step, carry):
+        @pl.when(jnp.logical_not(at_once))
+        def _():
+            finish_group(lax.rem(step + 1, groups))
+
+        return carry
+
+    lax.fori_loop(0, groups, back, 0)
 
     def finish(g, carry):
         @pl.when(has_high)
@@ -453,6 +714,14 @@
         @pl.when(has_low)
         def _():
             backward_copy(g).wait_send()
+
+        @pl.when(is_third)
+        def _():
+            skip_copy(g).wait_send()
+
+        @pl.when(jnp.logical_or(is_last, is_second))
+        def _():
+            mat_copy(g).wait_send()
 
         return carry
 
@@ -506,10 +775,17 @@
             vmem(*plane),
             vmem(*plane),
             vmem(*plane),
-            dma((7,)),
-            dma((2,)), dma((2,)), dma((2,)), dma((2,)),
-            dma((sectors,)), dma((sectors,)),
+            vmem(*plane),
+            vmem(nv, *plane),
+            vmem(nv, *plane),
+            vmem(nv, nv, planes, GROUP, cells),
+            vmem(*field),
+            dma((9,)),
+            dma((1,)), dma((1,)), dma((2,)), dma((2,)),
+            dma((sectors, groups)), dma((sectors, groups)),
             dma((groups,)), dma((groups,)), dma((groups,)), dma((groups,)),
+            dma((groups,)), dma((groups,)), dma((groups,)), dma((groups,)),
+            dma((groups,)), dma((groups,)), dma((planes,)),
             pltpu.SemaphoreType.REGULAR,
         ],
         compiler_params=pltpu.CompilerParams(collective_id=0, has_side_effects=True),

time: 33.1 us -> 26.3 us (0.79)
  Pallas kernels: 32.3 us -> 25.5 us
    pallas_call x1, Pallas kernels: 31.2 us -> 24.4 us  [per_device(): pl.pallas_call(functools.partial(kernel, sectors, slabs), out_shape=[vmem...]
where the time goes in v5:
time: 26.3 us; the launch traced here: 26.1 us
  Pallas kernels  25.5 us (97%)
  between operations  0.64 us (2%)
    pallas_call x1, Pallas kernels, per_device(): pl.pallas_call(functools.partial(kernel, sectors, slabs), out_shape=[vmem...  24.4 us
    pallas_call x1, Pallas kernels, per_device(): pl.pallas_call(write_out, out_shape=[jax.ShapeDtypeStruct(state.shape, jn...  1.07 us

profile of v5, /device:TPU:0, one launch (start us, length us, event | category | flops | bytes accessed | tf_op | source)
XLA Modules:
  0.0 26.1 jit_solution(10083124624812899903)
XLA Ops:
  0.6 24.4 %shard_map.77 = (f32[1,5,8,32,128]{4,3,2,1,0:T(8,128)S(1)}, f32[1,5,8,32,128]{4,3,2,1,0:T(8,128)S(1)}) custom-call(f32[1,5,8,32,128]{4,3,2,1,0:T(8,128)} %state.1, f32[1,5,8,32,128]{4,3,2,1,0:T(8,128)} %source.1, f32[1,5,5,8,32,128]{5,4,3,2,1,0:T(8,128)} %inverse.1, f32[5,1,5]{2,1,0:T(1,128)} %bitcast.4, f32[1,5,2,5]{3,2,1,0:T(2,128)} %bitcast.3, ...), custom_call_target="tpu_custom_call" | custom-call | tf_op jit(solution)/shard_map/pallas_call | solution.py:754
  25.0 1.1 %shard_map.78 = (f32[1,5,8,32,128]{4,3,2,1,0:T(8,128)}, f32[1,5,8,32,128]{4,3,2,1,0:T(8,128)}) custom-call(f32[1,5,8,32,128]{4,3,2,1,0:T(8,128)S(1)} %get-tuple-element.4.res_in, f32[1,5,8,32,128]{4,3,2,1,0:T(8,128)S(1)} %get-tuple-element.5.state_in), custom_call_target="tpu_custom_call" | custom-call | tf_op jit(solution)/shard_map/pallas_call | solution.py:794

commit v6 on v5

--- a/solution.py
+++ b/solution.py
@@ -364,7 +364,7 @@
         lax.fori_loop(0, planes, flux, 0)
 
     early = jnp.logical_or(jnp.logical_not(at_start), both(rotor, middle))
-    opens_at = jnp.where(early, 0, jnp.where(has_low, 3, 6))
+    opens_at = jnp.where(early, 0, 3)
     meets_at = jnp.where(at_start, 6, 1)
     passes_at = jnp.where(opens_at > 5, 7, 5)
     load_low.wait()

time: 26.3 us -> 26.3 us (level)
  no operation moved by 1% of the time
where the time goes in v6:
time: 26.3 us; the launch traced here: 26.1 us
  Pallas kernels  25.5 us (97%)
  between operations  0.64 us (2%)
    pallas_call x1, Pallas kernels, per_device(): pl.pallas_call(functools.partial(kernel, sectors, slabs), out_shape=[vmem...  24.4 us
    pallas_call x1, Pallas kernels, per_device(): pl.pallas_call(write_out, out_shape=[jax.ShapeDtypeStruct(state.shape, jn...  1.07 us

profile of v6, /device:TPU:0, one launch (start us, length us, event | category | flops | bytes accessed | tf_op | source)
XLA Modules:
  0.0 26.1 jit_solution(14617755086647752561)
XLA Ops:
  0.6 24.4 %shard_map.77 = (f32[1,5,8,32,128]{4,3,2,1,0:T(8,128)S(1)}, f32[1,5,8,32,128]{4,3,2,1,0:T(8,128)S(1)}) custom-call(f32[1,5,8,32,128]{4,3,2,1,0:T(8,128)} %state.1, f32[1,5,8,32,128]{4,3,2,1,0:T(8,128)} %source.1, f32[1,5,5,8,32,128]{5,4,3,2,1,0:T(8,128)} %inverse.1, f32[5,1,5]{2,1,0:T(1,128)} %bitcast.4, f32[1,5,2,5]{3,2,1,0:T(2,128)} %bitcast.3, ...), custom_call_target="tpu_custom_call" | custom-call | tf_op jit(solution)/shard_map/pallas_call | solution.py:754
  25.0 1.1 %shard_map.78 = (f32[1,5,8,32,128]{4,3,2,1,0:T(8,128)}, f32[1,5,8,32,128]{4,3,2,1,0:T(8,128)}) custom-call(f32[1,5,8,32,128]{4,3,2,1,0:T(8,128)S(1)} %get-tuple-element.4.res_in, f32[1,5,8,32,128]{4,3,2,1,0:T(8,128)S(1)} %get-tuple-element.5.state_in), custom_call_target="tpu_custom_call" | custom-call | tf_op jit(solution)/shard_map/pallas_call | solution.py:794
